TPU v7x, 8 devices: a whole 2x2x1 slice. The times are simulated.
8 devices in a mesh: dp: 1 (over z), tp: 2 (over y), sp: 4 (over x, core).
Axes of the slice: x: 2, y: 2, z: 1, core: 2. Of those that a mesh axis runs over, the one named last changes fastest.
Arguments:
- hidden: bfloat16 [16, 1536], P('dp')
- k_cache: bfloat16 [16, 8192, 12, 128], P('dp', 'sp', 'tp')
- v_cache: bfloat16 [16, 8192, 12, 128], P('dp', 'sp', 'tp')
- lengths: int32 [16], P('dp')
- rel_table: bfloat16 [8192, 12, 128], P('sp', 'tp')
- u_bias: bfloat16 [12, 128], P('tp')
- w_bias: bfloat16 [12, 128], P('tp')
- g_attn: bfloat16 [1536], replicated
- w_query: bfloat16 [1536, 12, 128], P(None, 'tp')
- w_key: bfloat16 [1536, 12, 128], P(None, 'tp')
- w_value: bfloat16 [1536, 12, 128], P(None, 'tp')
- w_out: bfloat16 [12, 128, 1536], P('tp')
- g_mlp: bfloat16 [1536], replicated
- w_up: bfloat16 [1536, 6144], P(None, 'tp')
- w_down: bfloat16 [6144, 1536], P('tp')
Outputs:
- output: bfloat16 [16, 1536], P('dp')
All inputs are finite; a program needn't handle non-finite values.
Results may differ from a plain program's by a relative error of at most 0.0124729.
Values sent between devices are 32-bit elements.
A program may use at most 1 GiB of HBM per device.

v0:
```python
import jax
import jax.numpy as jnp
from jax import lax
from jax.sharding import PartitionSpec as P

EPS = 1e-6
MASKED = -1e30


def rms_norm(tensor, gain):
    wide = tensor.astype(jnp.float32)
    mean_sq = jnp.mean(wide * wide, axis=-1, keepdims=True)
    return (wide * lax.rsqrt(mean_sq + EPS) * gain.astype(jnp.float32)).astype(jnp.bfloat16)


def distance_to_position(by_distance, first_pos, lengths, width):
    padded = jnp.pad(by_distance, ((0, 0), (0, 0), (width, 0)))
    starts = lengths - first_pos + 1
    taken = jax.vmap(lambda row, begin: lax.dynamic_slice_in_dim(row, begin, width, axis=1))(padded, starts)
    return jnp.flip(taken, axis=2)


def solution(mesh):
    spec_rows = P('dp', None)
    spec_cache = P('dp', 'sp', 'tp', None)
    in_specs = (spec_rows, spec_cache, spec_cache, P('dp'), P('sp', 'tp', None), P('tp', None), P('tp', None), P(None), P(None, 'tp', None), P(None, 'tp', None), P(None, 'tp', None), P('tp', None, None), P(None), P(None, 'tp'), P('tp', None))
    out_specs = spec_rows

    def layer_step(hidden, k_cache, v_cache, lengths, rel_table, u_bias, w_bias, g_attn, w_query, w_key, w_value, w_out, g_mlp, w_up, w_down):
        seq_blk = k_cache.shape[1]
        head_dim = k_cache.shape[3]
        first_pos = lax.axis_index('sp') * seq_blk
        normed = rms_norm(hidden, g_attn)
        query_vec = jnp.einsum('do,ojf->djf', normed, w_query, preferred_element_type=jnp.float32).astype(jnp.bfloat16)
        key_new = jnp.einsum('do,ojf->djf', normed, w_key, preferred_element_type=jnp.float32).astype(jnp.bfloat16)
        value_new = jnp.einsum('do,ojf->djf', normed, w_value, preferred_element_type=jnp.float32).astype(jnp.bfloat16)
        positions = first_pos + jnp.arange(seq_blk)
        write_mask = (positions[None, :] == lengths[:, None])[:, :, None, None]
        k_updated = jnp.where(write_mask, key_new[:, None], k_cache)
        v_updated = jnp.where(write_mask, value_new[:, None], v_cache)
        q_content = (query_vec.astype(jnp.float32) + u_bias.astype(jnp.float32)).astype(jnp.bfloat16)
        q_position = (query_vec.astype(jnp.float32) + w_bias.astype(jnp.float32)).astype(jnp.bfloat16)
        content = jnp.einsum('bhd,bshd->bhs', q_content, k_updated, preferred_element_type=jnp.float32)
        rel_local = jnp.einsum('bhd,shd->bhs', q_position, rel_table, preferred_element_type=jnp.float32)
        rel_all = lax.all_gather(rel_local, 'sp', axis=2, tiled=True)
        relative = distance_to_position(rel_all, first_pos, lengths, seq_blk)
        valid = (positions[None, :] <= lengths[:, None])[:, None, :]
        scores = jnp.where(valid, (content + relative) * (head_dim ** -0.5), MASKED)
        local_max = jnp.max(scores, axis=2)
        weights = jnp.where(valid, jnp.exp(scores - local_max[:, :, None]), 0.0)
        local_sum = jnp.sum(weights, axis=2)
        partial_ctx = jnp.einsum('bhs,bshd->bhd', weights.astype(jnp.bfloat16), v_updated, preferred_element_type=jnp.float32)
        packed = jnp.concatenate([partial_ctx, local_max[:, :, None], local_sum[:, :, None]], axis=2)
        gathered = lax.all_gather(packed, 'sp', axis=0)
        block_ctx = gathered[:, :, :, :head_dim]
        block_max = gathered[:, :, :, head_dim]
        block_sum = gathered[:, :, :, head_dim + 1]
        global_max = jnp.max(block_max, axis=0)
        rescale = jnp.exp(block_max - global_max[None])
        total = jnp.sum(rescale * block_sum, axis=0)
        context = (jnp.sum(rescale[:, :, :, None] * block_ctx, axis=0) / total[:, :, None]).astype(jnp.bfloat16)
        attn_part = jnp.einsum('bhd,hdm->bm', context, w_out, preferred_element_type=jnp.float32)
        attn_out = lax.psum(attn_part, 'tp')
        resid_mid = (hidden.astype(jnp.float32) + attn_out).astype(jnp.bfloat16)
        normed_mlp = rms_norm(resid_mid, g_mlp)
        up_proj = jnp.dot(normed_mlp, w_up, preferred_element_type=jnp.float32)
        activated = jax.nn.gelu(up_proj, approximate=True).astype(jnp.bfloat16)
        down_part = jnp.dot(activated, w_down, preferred_element_type=jnp.float32)
        down_proj = lax.psum(down_part, 'tp')
        hidden_out = (resid_mid.astype(jnp.float32) + down_proj).astype(jnp.bfloat16)
        return hidden_out

    return jax.shard_map(layer_step, mesh=mesh, in_specs=in_specs, out_specs=out_specs, check_vma=False)
```

profile of v0, /device:TPU:0, one launch (start us, length us, event | category | flops | bytes accessed | tf_op | source)
XLA Modules:
  0.0 179.1 jit_solution(5979999905762340794)
XLA Ops:
  6.6 0.8 convert_element_type.63
  7.4 1.0 fusion.24
  8.5 0.7 convert_element_type.70
  9.2 2.1 %fusion.8 = f32[16,6,128]{2,0,1:T(8,128)S(1)} fusion(bf16[1536,6,128]{2,0,1:T(8,128)(2,1)} %param.23, bf16[16,1536]{1,0:T(8,128)(2,1)} %param.15, f32[1536]{0:T(1024)S(1)} %convert_element_type.63, f32[16]{0:T(128)S(1)} %add_rsqrt_fusion.1), kind=kOutput, calls=%fused_computation.16 | convolution fusion | flops 37871616 | bytes 2463808 | tf_op jit(solution)/shard_map/do,ojf->djf/dot_general | solution.py:34
  11.3 1.8 %convolution_bitcast_fusion = f32[16,6,2048]{2,0,1:T(8,128)} fusion(bf16[2048,6,128]{2,0,1:T(8,128)(2,1)S(1)} %copy-done, f32[16,6,128]{2,0,1:T(8,128)S(1)} %fusion.8, f32[6,128]{1,0:T(8,128)S(1)} %convert_element_type.70), kind=kOutput, calls=%fused_computation.11 | convolution fusion | flops 50356224 | bytes 3984384 | tf_op jit(solution)/shard_map/bhd,shd->bhs/dot_general | solution.py:44
  13.2 2.2 %convolution_convert_fusion.1 = bf16[16,6,128]{2,0,1:T(8,128)(2,1)S(1)} fusion(bf16[1536,6,128]{2,0,1:T(8,128)(2,1)} %param.24, bf16[16,1536]{1,0:T(8,128)(2,1)} %param.15, f32[1536]{0:T(1024)S(1)} %convert_element_type.63, f32[16]{0:T(128)S(1)} %add_rsqrt_fusion.1), kind=kOutput, calls=%fused_computation.14 | convolution fusion | flops 37859328 | bytes 2439232 | tf_op jit(solution)/shard_map/do,ojf->djf/dot_general | solution.py:35
  15.4 2.1 %convolution_convert_fusion = bf16[16,6,128]{2,0,1:T(8,128)(2,1)S(1)} fusion(bf16[1536,6,128]{2,0,1:T(8,128)(2,1)} %param.25, bf16[16,1536]{1,0:T(8,128)(2,1)S(1)} %copy-done.3, f32[1536]{0:T(1024)S(1)} %convert_element_type.63, f32[16]{0:T(128)S(1)} %add_rsqrt_fusion.1), kind=kOutput, calls=%fused_computation.13 | convolution fusion | flops 37859328 | bytes 2439232 | tf_op jit(solution)/shard_map/do,ojf->djf/dot_general | solution.py:36
  17.8 21.4 %fusion.2 = f32[16,6,1,2048]{3,2,1,0:T(1,128)S(1)} fusion(bf16[16,2048,6,128]{3,1,2,0:T(8,128)(2,1)} %param.16, pred[16,2048]{1,0:T(8,128)(4,1)S(1)} %get-tuple-element.51, bf16[16,6,128]{2,1,0:T(8,128)(2,1)S(1)} %copy.35, bf16[16,6,128,1]{2,0,1,3:T(8,128)(2,1)S(1)} %fusion.50), kind=kOutput, calls=%fused_computation.5 | convolution fusion | flops 75497472 | bytes 51200000 | tf_op jit(solution)/shard_map/bhd,bshd->bhs/dot_general | solution.py:43
  39.2 2.4 %all-gather.3.cloned.1.call-done = f32[16,6,8192]{2,0,1:T(8,128)} async-done(((f32[16,6,2048]{2,0,1:T(8,128)}), f32[16,6,8192]{2,0,1:T(8,128)}) %all-gather.3.cloned.1.call-update) | async-done | bytes 3145744 | tf_op jit(solution)/shard_map/all_gather | solution.py:45
  41.6 4.2 %pad.5 = f32[16,6,10240]{2,0,1:T(8,128)} pad(f32[16,6,8192]{2,0,1:T(8,128)} %all-gather.3.cloned.1.call-done, f32[]{:T(128)} %constant.17.clone.1), padding=0_0x0_0x2048_0 | pad | bytes 7077892 | tf_op jit(solution)/shard_map/jit(_pad)/pad | solution.py:17
  45.7 49.5 %while.2 = (s32[]{:T(128)}, f32[16,6,10240]{2,0,1:T(8,128)}, s32[16,3]{0,1:T(4,128)S(1)}, f32[16,6,2048]{2,1,0:T(8,128)S(1)}) while((s32[]{:T(128)}, f32[16,6,10240]{2,0,1:T(8,128)}, s32[16,3]{0,1:T(4,128)S(1)}, f32[16,6,2048]{2,1,0:T(8,128)S(1)}) %tuple.33), condition=%wide.while_cond.clone, body=%wide.while_body.sunk.clone | while | flops 2 | bytes 213109 | solution.py:19
  46.4 2.4 %constant_dynamic-slice_fusion.7 = f32[1,6,2048]{2,0,1:T(1,128)S(1)} fusion(f32[16,6,10240]{2,0,1:T(8,128)} %get-tuple-element.102, s32[]{:T(128)} %bitcast.46, s32[]{:T(128)} %bitcast.47), kind=kLoop, calls=%fused_computation.2.clone.1.clone | loop fusion | bytes 98312 | tf_op jit(solution)/shard_map/vmap()/gather
  48.9 0.5 fusion.73
  49.5 2.4 %constant_dynamic-slice_fusion.7 = f32[1,6,2048]{2,0,1:T(1,128)S(1)} fusion(f32[16,6,10240]{2,0,1:T(8,128)} %get-tuple-element.102, s32[]{:T(128)} %bitcast.46, s32[]{:T(128)} %bitcast.47), kind=kLoop, calls=%fused_computation.2.clone.1.clone | loop fusion | bytes 98312 | tf_op jit(solution)/shard_map/vmap()/gather
  52.6 2.4 %constant_dynamic-slice_fusion.7 = f32[1,6,2048]{2,0,1:T(1,128)S(1)} fusion(f32[16,6,10240]{2,0,1:T(8,128)} %get-tuple-element.102, s32[]{:T(128)} %bitcast.46, s32[]{:T(128)} %bitcast.47), kind=kLoop, calls=%fused_computation.2.clone.1.clone | loop fusion | bytes 98312 | tf_op jit(solution)/shard_map/vmap()/gather
  55.1 0.5 fusion.73
  55.6 2.4 %constant_dynamic-slice_fusion.7 = f32[1,6,2048]{2,0,1:T(1,128)S(1)} fusion(f32[16,6,10240]{2,0,1:T(8,128)} %get-tuple-element.102, s32[]{:T(128)} %bitcast.46, s32[]{:T(128)} %bitcast.47), kind=kLoop, calls=%fused_computation.2.clone.1.clone | loop fusion | bytes 98312 | tf_op jit(solution)/shard_map/vmap()/gather
  58.2 0.5 fusion.73
  58.7 2.4 %constant_dynamic-slice_fusion.7 = f32[1,6,2048]{2,0,1:T(1,128)S(1)} fusion(f32[16,6,10240]{2,0,1:T(8,128)} %get-tuple-element.102, s32[]{:T(128)} %bitcast.46, s32[]{:T(128)} %bitcast.47), kind=kLoop, calls=%fused_computation.2.clone.1.clone | loop fusion | bytes 98312 | tf_op jit(solution)/shard_map/vmap()/gather
  61.3 0.5 fusion.73
  61.8 2.4 %constant_dynamic-slice_fusion.7 = f32[1,6,2048]{2,0,1:T(1,128)S(1)} fusion(f32[16,6,10240]{2,0,1:T(8,128)} %get-tuple-element.102, s32[]{:T(128)} %bitcast.46, s32[]{:T(128)} %bitcast.47), kind=kLoop, calls=%fused_computation.2.clone.1.clone | loop fusion | bytes 98312 | tf_op jit(solution)/shard_map/vmap()/gather
  64.4 0.5 fusion.73
  64.9 2.4 %constant_dynamic-slice_fusion.7 = f32[1,6,2048]{2,0,1:T(1,128)S(1)} fusion(f32[16,6,10240]{2,0,1:T(8,128)} %get-tuple-element.102, s32[]{:T(128)} %bitcast.46, s32[]{:T(128)} %bitcast.47), kind=kLoop, calls=%fused_computation.2.clone.1.clone | loop fusion | bytes 98312 | tf_op jit(solution)/shard_map/vmap()/gather
  67.5 0.5 fusion.73
  68.0 2.4 %constant_dynamic-slice_fusion.7 = f32[1,6,2048]{2,0,1:T(1,128)S(1)} fusion(f32[16,6,10240]{2,0,1:T(8,128)} %get-tuple-element.102, s32[]{:T(128)} %bitcast.46, s32[]{:T(128)} %bitcast.47), kind=kLoop, calls=%fused_computation.2.clone.1.clone | loop fusion | bytes 98312 | tf_op jit(solution)/shard_map/vmap()/gather
  70.6 0.5 fusion.73
  71.1 2.4 %constant_dynamic-slice_fusion.7 = f32[1,6,2048]{2,0,1:T(1,128)S(1)} fusion(f32[16,6,10240]{2,0,1:T(8,128)} %get-tuple-element.102, s32[]{:T(128)} %bitcast.46, s32[]{:T(128)} %bitcast.47), kind=kLoop, calls=%fused_computation.2.clone.1.clone | loop fusion | bytes 98312 | tf_op jit(solution)/shard_map/vmap()/gather
  73.7 0.5 fusion.73
  74.2 2.4 %constant_dynamic-slice_fusion.7 = f32[1,6,2048]{2,0,1:T(1,128)S(1)} fusion(f32[16,6,10240]{2,0,1:T(8,128)} %get-tuple-element.102, s32[]{:T(128)} %bitcast.46, s32[]{:T(128)} %bitcast.47), kind=kLoop, calls=%fused_computation.2.clone.1.clone | loop fusion | bytes 98312 | tf_op jit(solution)/shard_map/vmap()/gather
  77.3 2.4 %constant_dynamic-slice_fusion.7 = f32[1,6,2048]{2,0,1:T(1,128)S(1)} fusion(f32[16,6,10240]{2,0,1:T(8,128)} %get-tuple-element.102, s32[]{:T(128)} %bitcast.46, s32[]{:T(128)} %bitcast.47), kind=kLoop, calls=%fused_computation.2.clone.1.clone | loop fusion | bytes 98312 | tf_op jit(solution)/shard_map/vmap()/gather
  80.4 2.4 %constant_dynamic-slice_fusion.7 = f32[1,6,2048]{2,0,1:T(1,128)S(1)} fusion(f32[16,6,10240]{2,0,1:T(8,128)} %get-tuple-element.102, s32[]{:T(128)} %bitcast.46, s32[]{:T(128)} %bitcast.47), kind=kLoop, calls=%fused_computation.2.clone.1.clone | loop fusion | bytes 98312 | tf_op jit(solution)/shard_map/vmap()/gather
  83.5 2.4 %constant_dynamic-slice_fusion.7 = f32[1,6,2048]{2,0,1:T(1,128)S(1)} fusion(f32[16,6,10240]{2,0,1:T(8,128)} %get-tuple-element.102, s32[]{:T(128)} %bitcast.46, s32[]{:T(128)} %bitcast.47), kind=kLoop, calls=%fused_computation.2.clone.1.clone | loop fusion | bytes 98312 | tf_op jit(solution)/shard_map/vmap()/gather
  86.0 0.5 fusion.73
  86.6 2.4 %constant_dynamic-slice_fusion.7 = f32[1,6,2048]{2,0,1:T(1,128)S(1)} fusion(f32[16,6,10240]{2,0,1:T(8,128)} %get-tuple-element.102, s32[]{:T(128)} %bitcast.46, s32[]{:T(128)} %bitcast.47), kind=kLoop, calls=%fused_computation.2.clone.1.clone | loop fusion | bytes 98312 | tf_op jit(solution)/shard_map/vmap()/gather
  89.1 0.5 fusion.73
  89.7 2.4 %constant_dynamic-slice_fusion.7 = f32[1,6,2048]{2,0,1:T(1,128)S(1)} fusion(f32[16,6,10240]{2,0,1:T(8,128)} %get-tuple-element.102, s32[]{:T(128)} %bitcast.46, s32[]{:T(128)} %bitcast.47), kind=kLoop, calls=%fused_computation.2.clone.1.clone | loop fusion | bytes 98312 | tf_op jit(solution)/shard_map/vmap()/gather
  92.2 0.5 fusion.73
  92.8 2.4 %constant_dynamic-slice_fusion.7 = f32[1,6,2048]{2,0,1:T(1,128)S(1)} fusion(f32[16,6,10240]{2,0,1:T(8,128)} %get-tuple-element.102, s32[]{:T(128)} %bitcast.46, s32[]{:T(128)} %bitcast.47), kind=kLoop, calls=%fused_computation.2.clone.1.clone | loop fusion | bytes 98312 | tf_op jit(solution)/shard_map/vmap()/gather
  95.2 1.5 rev.4
  97.3 1.4 fusion.14
  99.1 18.6 %fusion = f32[16,6,1,128]{3,2,1,0:T(1,128)S(1)} fusion(bf16[16,2048,6,128]{3,1,2,0:T(8,128)(2,1)} %param.17, pred[16,2048]{1,0:T(8,128)(4,1)S(1)} %get-tuple-element.51, bf16[16,6,128]{2,1,0:T(8,128)(2,1)S(1)} %copy.37, bf16[16,6,2048,1]{2,1,0,3:T(8,128)(2,1)} %get-tuple-element.48), kind=kOutput, calls=%fused_computation.3 | convolution fusion | flops 75497472 | bytes 50831360 | tf_op jit(solution)/shard_map/bhs,bshd->bhd/dot_general | solution.py:52
  117.8 8.9 %all-gather = f32[64,6,130]{2,0,1:T(8,128)S(1)} all-gather(f32[16,6,130]{2,0,1:T(8,128)S(1)} %pad_maximum_fusion), channel_id=2, replica_groups=mesh['dp'=1,'tp'=2,'sp'=4] {'sp'}, dimensions={0}, use_global_device_ids=true | all-gather | bytes 249600 | tf_op jit(solution)/shard_map/all_gather | solution.py:54
  127.3 1.1 convolution_bitcast_fusion.1
  128.5 16.1 %all-reduce.5.cloned.1.call-done = f32[16,1536]{1,0:T(8,128)} async-done(((f32[16,1536]{1,0:T(8,128)}), f32[16,1536]{1,0:T(8,128)}) %all-reduce.5.cloned.1.call-update) | async-done | bytes 98320 | tf_op jit(solution)/shard_map/psum | solution.py:63
  144.6 1.0 fusion.28
  145.6 9.8 %fusion.32 = f32[16,1536]{1,0:T(8,128)} fusion(bf16[3072,1536]{1,0:T(8,128)(2,1)} %param.29, bf16[1536,3072]{1,0:T(8,128)(2,1)} %param.28, bf16[16,1536]{1,0:T(8,128)(2,1)S(1)} %get-tuple-element.45, f32[1536]{0:T(1024)S(1)} %convert_element_type.77, f32[16]{0:T(128)S(1)} %add_rsqrt_fusion), kind=kOutput, calls=%fused_computation.54 | convolution fusion | flops 302530560 | bytes 19028032 | tf_op jit(solution)/shard_map/dot_general | solution.py:68
  155.4 15.6 %all-reduce.7.cloned.1.call-done = f32[16,1536]{1,0:T(8,128)} async-done(((f32[16,1536]{1,0:T(8,128)}), f32[16,1536]{1,0:T(8,128)}) %all-reduce.7.cloned.1.call-update) | async-done | bytes 98320 | tf_op jit(solution)/shard_map/psum | solution.py:69
  171.0 1.5 fusion.31
  (79 shorter events, 6.3 us)
Async XLA Ops:
  6.5 4.8 %copy-start = (bf16[2048,6,128]{2,0,1:T(8,128)(2,1)S(1)}, bf16[2048,6,128]{2,0,1:T(8,128)(2,1)}, u32[]{:S(2)}) copy-start(bf16[2048,6,128]{2,0,1:T(8,128)(2,1)} %param.19) | copy-start | bytes 9437188
  6.5 8.9 %copy-start.3 = (bf16[16,1536]{1,0:T(8,128)(2,1)S(1)}, bf16[16,1536]{1,0:T(8,128)(2,1)}, u32[]{:S(2)}) copy-start(bf16[16,1536]{1,0:T(8,128)(2,1)} %param.15) | copy-start | bytes 147460
  6.5 8.9 %copy-start.5 = (bf16[6,128]{1,0:T(8,128)(2,1)S(1)}, bf16[6,128]{1,0:T(8,128)(2,1)}, u32[]{:S(2)}) copy-start(bf16[6,128]{1,0:T(8,128)(2,1)} %param.20) | copy-start | bytes 4612
  6.5 11.0 %copy-start.6 = (s32[16]{0:T(128)S(1)}, s32[16]{0:T(128)}, u32[]{:S(2)}) copy-start(s32[16]{0:T(128)} %param.18) | copy-start | bytes 196
  6.5 35.1 %all-gather.3.cloned.1.call-start = ((), (), s32[]{:S(2)}) async-start(), calls=%async_computation | async-start | bytes 3932160 | tf_op jit(solution)/shard_map/all_gather | solution.py:45
  13.2 131.4 %all-reduce.5.cloned.1.call-start = ((), (), s32[]{:S(2)}) async-start(), calls=%async_computation.1 | async-start | bytes 196608 | tf_op jit(solution)/shard_map/psum | solution.py:63
  99.1 28.2 %copy-start.2 = (bf16[6,128,1536]{2,1,0:T(8,128)(2,1)S(1)}, bf16[6,128,1536]{2,1,0:T(8,128)(2,1)}, u32[]{:S(2)}) copy-start(bf16[6,128,1536]{2,1,0:T(8,128)(2,1)} %param.26) | copy-start | bytes 7077892
  99.1 29.4 %copy-start.4 = (bf16[1536]{0:T(1024)(128)(2,1)S(1)}, bf16[1536]{0:T(1024)(128)(2,1)}, u32[]{:S(2)}) copy-start(bf16[1536]{0:T(1024)(128)(2,1)} %param.27) | copy-start | bytes 9220
  128.4 42.6 %all-reduce.7.cloned.1.call-start = ((), (), s32[]{:S(2)}) async-start(), calls=%async_computation.2 | async-start | bytes 196608 | tf_op jit(solution)/shard_map/psum | solution.py:69
  145.6 26.9 %copy-start.1 = (bf16[2048,6,128]{2,0,1:T(8,128)(2,1)S(1)}, bf16[2048,6,128]{2,0,1:T(8,128)(2,1)}, u32[]{:S(2)}) copy-start(bf16[2048,6,128]{2,0,1:T(8,128)(2,1)} %param.19) | copy-start | bytes 9437188
Sparse Core Ops, SparseCore 0:
  13.3 28.2 all-gather.2
  128.5 16.0 all-reduce.4
  155.5 15.4 all-reduce.6
where the time goes:
time: 181 us; the launch traced here: 179 us
  matrix products  59.1 us (33%)
  local copies, waits for them, and re-layouts  55.2 us (30%)
  waiting for transfers between devices  34.2 us (19%)
  between operations  13.3 us (7%)
  blocking collectives  8.91 us (5%)
  other arithmetic  7.89 us (4%)
    gather x64, local copies, waits for them, and re-layouts  49.1 us
    dot_general x1, matrix products, layer_step(): jnp.einsum('bhd,bshd->bhs', q_content, k_updated, preferred_element_type=...  21.4 us
    dot_general x1, matrix products, layer_step(): jnp.einsum('bhs,bshd->bhd', weights.astype(jnp.bfloat16), v_updated, pref...  18.6 us
    psum x1, waiting for transfers between devices, layer_step(): attn_out = lax.psum(attn_part, 'tp')  16.1 us
    psum x1, waiting for transfers between devices, layer_step(): down_proj = lax.psum(down_part, 'tp')  15.6 us
    dot_general x1, matrix products, layer_step(): down_part = jnp.dot(activated, w_down, preferred_element_type=jnp.float32)  9.75 us
    all_gather x1, blocking collectives, layer_step(): gathered = lax.all_gather(packed, 'sp', axis=0)  8.91 us
    pad x1, local copies, waits for them, and re-layouts, distance_to_position(): padded = jnp.pad(by_distance, ((0, 0), (0, 0), (width, 0)))  4.15 us
  transfers between devices with their start and end apart: 3, of which 3 were waited for; matrix products, arithmetic and copies ran while one was open for 14% of the time, Pallas kernels for 0%

commit v1 on v0

v1 whole, which is shorter than its diff:
```python
import functools

import jax
import jax.numpy as jnp
from jax import lax
from jax.experimental import pallas as pl
from jax.experimental.pallas import tpu as pltpu
from jax.sharding import PartitionSpec as P

EPS = 1e-6
MASKED = -1e30
MESH = pl.DeviceIdType.MESH
F32 = jnp.float32
BF16 = jnp.bfloat16
VMEM = pltpu.VMEM
NT = (((1,), (1,)), ((), ()))

BATCH, HEADS, HEAD, BLK, D = 16, 6, 128, 2048, 1536
TILES = BLK // 128
GROUPS, PER = 4, 4
GROWS = HEADS * PER
ROWS = GROUPS * GROWS
RING = 10
HID = 768


def rms_norm(wide, gain):
    mean_sq = jnp.mean(wide * wide, axis=-1, keepdims=True)
    return (wide * lax.rsqrt(mean_sq + EPS) * gain).astype(BF16)


def row_lengths(len_ref, group):
    seq = lax.rem(lax.broadcasted_iota(jnp.int32, (GROWS, 128), 0), PER)
    out = jnp.full((GROWS, 128), len_ref[PER * group], jnp.int32)
    for i in range(1, PER):
        out = jnp.where(seq == i, len_ref[PER * group + i], out)
    return out


def front_kernel(len_ref, x_ref, g_ref, u_ref, wb_ref, wq_hbm, wk_hbm, wv_hbm, rel_hbm,
                 qr_ref, rolled_ref, aux_ref, wq, wk, wv, rel, qf, raw, sems):
    copies = {}
    for h in range(HEADS):
        for j, (src, dst) in enumerate(((wq_hbm, wq), (rel_hbm, rel), (wk_hbm, wk), (wv_hbm, wv))):
            copies[j, h] = pltpu.make_async_copy(src.at[h], dst.at[h], sems.at[j, h])
    for j in range(4):
        for h in range(HEADS):
            copies[j, h].start()
    normed = rms_norm(x_ref[...].astype(F32), g_ref[...].astype(F32))
    qf[...] = jnp.zeros_like(qf)
    q_content = []
    for h in range(HEADS):
        copies[0, h].wait()
        q = jnp.dot(normed, wq[h], preferred_element_type=F32).astype(BF16).astype(F32)
        qc = (q + u_ref[h : h + 1, :].astype(F32)).astype(BF16).astype(F32)
        qp = (q + wb_ref[h : h + 1, :].astype(F32)).astype(BF16)
        q_content.append(qc)
        for s in range(GROUPS):
            row = s * GROWS + h * PER
            qf[row : row + PER, h * 128 : h * 128 + 128] = qc[s * PER : s * PER + PER, :]
        copies[1, h].wait()
        by_dist = lax.dot_general(qp, rel[h], NT, preferred_element_type=F32)
        for c in range(TILES):
            for s in range(GROUPS):
                row = s * GROWS + h * PER
                raw[c, row : row + PER, :] = by_dist[s * PER : s * PER + PER, c * 128 : c * 128 + 128]
    qr_ref[...] = qf[...].astype(BF16)
    lane = lax.broadcasted_iota(jnp.int32, (GROWS, 128), 1)
    for s in range(GROUPS):
        n = row_lengths(len_ref, s)
        r = lax.rem(n, BLK)
        big, small = lax.div(r, 128), lax.rem(r, 128)
        aux_ref[2, s * GROWS : s * GROWS + GROWS, :] = n.astype(F32)
        for t in range(GROWS // 8):
            sl = slice(8 * t, 8 * t + 8)
            row = s * GROWS + 8 * t
            idx = lax.rem(small[sl] - lane[sl] + 128, 128)
            tiles = [jnp.take_along_axis(raw[(TILES - c) % TILES, row : row + 8, :], idx, axis=1) for c in range(TILES)]
            for k in range(4):
                bit = lax.rem(lax.div(big[sl], 1 << k), 2) == 1
                tiles = [jnp.where(bit, tiles[(c - (1 << k)) % TILES], tiles[c]) for c in range(TILES)]
            low = lane[sl] <= small[sl]
            for c in range(TILES):
                rolled_ref[c, row : row + 8, :] = jnp.where(low, tiles[c], tiles[(c + 1) % TILES])
    for h in range(HEADS):
        copies[2, h].wait()
        kn = jnp.dot(normed, wk[h], preferred_element_type=F32).astype(BF16).astype(F32)
        copies[3, h].wait()
        vn = jnp.dot(normed, wv[h], preferred_element_type=F32).astype(BF16).astype(F32)
        sn = jnp.broadcast_to(jnp.sum(q_content[h] * kn, axis=1, keepdims=True), (BATCH, 128))
        for s in range(GROUPS):
            row = s * GROWS + h * PER
            aux_ref[0, row : row + PER, :] = sn[s * PER : s * PER + PER, :]
            aux_ref[1, row : row + PER, :] = vn[s * PER : s * PER + PER, :]


def main_kernel(k_hbm, v_hbm, qr_ref, rolled, aux, x_ref, g_ref, wo_hbm, wu_hbm, wd_hbm, out_ref,
                ring, wo, wu, wd, acc, score, from_pair, to_far, from_far, stat_out, stat_in, ctx, ctx_out, ctx_in,
                part_out, part_in, x1_ref, mlp_out, mlp_in, fin_out, fin_in,
                ring_sem, w_sem, pair_s, pair_r, far_s, far_r, stat_s, stat_r, ctx_s, ctx_r,
                part_s, part_r, mlp_s, mlp_r, fin_s, fin_r):
    tp, sp = lax.axis_index("tp"), lax.axis_index("sp")
    me = tp * 4 + sp
    odd = lax.rem(sp, 2)
    pair = sp + 1 - 2 * odd

    def load(step, slot):
        @pl.when(step < BATCH)
        def _():
            pltpu.make_async_copy(k_hbm.at[step], ring.at[slot], ring_sem.at[slot]).start()

        @pl.when(jnp.logical_and(step >= BATCH, step < 2 * BATCH))
        def _():
            pltpu.make_async_copy(v_hbm.at[step - BATCH], ring.at[slot], ring_sem.at[slot]).start()

    for i in range(RING):
        pltpu.make_async_copy(k_hbm.at[i], ring.at[i], ring_sem.at[i]).start()

    others = [(dt, ds) for dt in range(2) for ds in range(4) if (dt, ds) != (0, 0)]

    def peer(dt, ds):
        return lax.rem(tp + dt, 2), lax.rem(sp + ds, 4)

    def source(dt, ds):
        return lax.rem(tp + 2 - dt, 2), lax.rem(sp + 4 - ds, 4)

    barrier = pltpu.get_barrier_semaphore()
    for dt, ds in others:
        t, s = peer(dt, ds)
        pl.semaphore_signal(barrier, inc=1, device_id={"tp": t, "sp": s}, device_id_type=MESH)
    pl.semaphore_wait(barrier, 7)

    def remote(src, dst, send, recv, t, s):
        return pltpu.make_async_remote_copy(
            src_ref=src, dst_ref=dst, send_sem=send, recv_sem=recv, device_id={"tp": t, "sp": s}, device_id_type=MESH
        )

    def rows(g):
        return pl.ds(g * GROWS, GROWS)

    def pair_copy(g):
        return remote(rolled.at[:, rows(g), :], from_pair.at[:, rows(g), :], pair_s.at[g], pair_r.at[g], tp, pair)

    def far_copy(g):
        return remote(to_far.at[:, rows(g), :], from_far.at[:, rows(g), :], far_s.at[g], far_r.at[g], tp, 3 - sp)

    for g in range(GROUPS):
        pair_copy(g).start()

    lane = lax.broadcasted_iota(jnp.int32, (GROWS, 128), 1)
    row_id = lax.broadcasted_iota(jnp.int32, (128, 256), 0)
    row_seq = lax.div(row_id, GROWS) * PER + lax.rem(row_id, PER)
    acc[...] = jnp.zeros_like(acc)

    def k_step(b, _):
        slot = lax.rem(b, RING)
        pltpu.make_async_copy(k_hbm.at[b], ring.at[slot], ring_sem.at[slot]).wait()
        total = None
        for p in range(HEADS // 2):
            keys = jnp.concatenate([ring[slot, 2 * p], ring[slot, 2 * p + 1]], axis=1)
            query = jnp.where(row_seq == b, qr_ref[:, 256 * p : 256 * p + 256], jnp.zeros((), BF16))
            dots = lax.dot_general(keys, query, NT, preferred_element_type=F32)
            total = dots if total is None else total + dots
        acc[...] += total
        load(b + RING, slot)

        @pl.when(b == 2)
        def _():
            for g in range(GROUPS):
                pair_copy(g).wait()
                n = aux[2, g * GROWS : g * GROWS + GROWS, :].astype(jnp.int32)
                r = lax.rem(n, BLK)
                last = lax.div(n, BLK) == 3
                for c in range(TILES):
                    mine = jnp.logical_or(jnp.logical_and(last, lane + 128 * c <= r), odd == 0)
                    to_far[c, g * GROWS : g * GROWS + GROWS, :] = jnp.where(
                        mine, rolled[c, g * GROWS : g * GROWS + GROWS, :], from_pair[c, g * GROWS : g * GROWS + GROWS, :]
                    )

        @pl.when(b == 3)
        def _():
            for g in range(GROUPS):
                far_copy(g).start()

        return 0

    lax.fori_loop(0, BATCH, k_step, 0)

    weights = (
        pltpu.make_async_copy(wo_hbm, wo, w_sem.at[0]),
        pltpu.make_async_copy(wu_hbm.at[:, pl.ds(pl.multiple_of(sp * HID, 128), HID)], wu, w_sem.at[1]),
        pltpu.make_async_copy(wd_hbm.at[pl.ds(pl.multiple_of(sp * HID, 128), HID), :], wd, w_sem.at[2]),
    )
    for w in weights:
        w.start()
    for c in range(TILES):
        score[c] = jnp.transpose(acc[128 * c : 128 * c + 128, :])[:ROWS]

    def softmax(g):
        base = pl.multiple_of(g * GROWS, 8)
        sl = pl.ds(base, GROWS)
        far_copy(g).wait()
        n = aux[2, sl, :].astype(jnp.int32)
        new = aux[0, sl, :]
        r = lax.rem(n, BLK)
        block = lax.div(n, BLK) - sp
        here = n - sp * BLK
        top = jnp.full((GROWS, 128), MASKED, F32)
        for c in range(TILES):
            pos = lane + 128 * c
            owner = jnp.where(pos <= r, block, block - 1)
            rel = jnp.where(owner == sp, rolled[c, sl, :], jnp.where(owner == pair, from_pair[c, sl, :], from_far[c, sl, :]))
            content = jnp.where(pos == here, new, score[c, sl, :])
            sc = jnp.where(pos <= here, (content + rel) * (HEAD**-0.5), MASKED)
            score[c, sl, :] = sc
            top = jnp.maximum(top, sc)
        top = jnp.max(top, axis=1, keepdims=True)
        total = jnp.zeros((GROWS, 128), F32)
        at_new = jnp.zeros((GROWS, 128), F32)
        for c in range(TILES):
            pos = lane + 128 * c
            w = jnp.where(pos <= here, jnp.exp(score[c, sl, :] - top), 0.0)
            total = total + w
            at_new = at_new + jnp.where(pos == here, w.astype(BF16).astype(F32), 0.0)
            score[c, sl, :] = jnp.where(pos == here, 0.0, w)
        total = jnp.sum(total, axis=1, keepdims=True)
        at_new = jnp.sum(at_new, axis=1, keepdims=True)
        stat_out[sl, :] = jnp.where(lane < 64, top, total)
        ctx_out_scale = jnp.broadcast_to(at_new, (GROWS, 128))
        acc[sl, :] = ctx_out_scale

    def stat_copy(ds):
        t, s = peer(0, ds)
        return remote(stat_out, stat_in.at[ds - 1], stat_s.at[ds - 1], stat_r.at[ds - 1], t, s)

    head_row = lax.broadcasted_iota(jnp.int32, (HEADS, 128), 0)

    def v_step(b, _):
        g, i = lax.div(b, PER), lax.rem(b, PER)

        @pl.when(i == 0)
        def _():
            softmax(g)

        slot = lax.rem(b + BATCH, RING)
        pltpu.make_async_copy(v_hbm.at[b], ring.at[slot], ring_sem.at[slot]).wait()
        first = g * GROWS + i
        probs = jnp.concatenate([score[c, pl.ds(first, HEADS, stride=PER), :] for c in range(TILES)], axis=1).astype(BF16)
        out = jnp.zeros((HEADS, 128), F32)
        for h in range(HEADS):
            dots = jnp.dot(probs, ring[slot, h], preferred_element_type=F32)
            out = jnp.where(head_row == h, dots, out)
        ctx[pl.ds(first, HEADS, stride=PER), :] = out
        load(b + BATCH + RING, slot)

        @pl.when(b == BATCH - PER)
        def _():
            for ds in range(1, 4):
                stat_copy(ds).start()

        return 0

    lax.fori_loop(0, BATCH, v_step, 0)

    for ds in range(1, 4):
        stat_copy(ds).wait()
    mine = stat_out[...]
    top, total = mine[:, :1], mine[:, 64:65]
    all_top = top
    for ds in range(3):
        all_top = jnp.maximum(all_top, stat_in[ds, :, :1])
    all_total = total * jnp.exp(top - all_top)
    for ds in range(3):
        all_total = all_total + stat_in[ds, :, 64:65] * jnp.exp(stat_in[ds, :, :1] - all_top)
    scale = jnp.exp(top - all_top) / all_total
    scaled = (ctx[...] + acc[:ROWS, :] * aux[1]) * scale
    for g in range(GROUPS):
        ctx_out[g] = scaled[g * GROWS : g * GROWS + GROWS, :]

    def ctx_copy(ds):
        t, s = peer(0, ds)
        return remote(ctx_out.at[s], ctx_in.at[ds], ctx_s.at[ds - 1], ctx_r.at[ds - 1], t, s)

    for ds in range(1, 4):
        ctx_copy(ds).start()
    for w in weights:
        w.wait()
    ctx_in[0] = ctx_out[sp]
    for ds in range(1, 4):
        ctx_copy(ds).wait()
    whole = ((ctx_in[0] + ctx_in[1]) + (ctx_in[2] + ctx_in[3])).astype(BF16).astype(F32)
    lhs = jnp.concatenate([whole[h * PER : h * PER + PER, :] for h in range(HEADS)], axis=1).astype(BF16)
    part_out[...] = jnp.dot(lhs, wo[...], preferred_element_type=F32)

    def part_copy(j, sending):
        t, s = peer(*others[j])
        ft, fs = source(*others[j])
        slot = me if sending else ft * 4 + fs
        return remote(part_out, part_in.at[slot], part_s.at[j], part_r.at[j], t, s)

    for j in range(7):
        part_copy(j, True).start()
    part_in[me] = part_out[...]
    for j in range(7):
        part_copy(j, True).wait_send()
        part_copy(j, False).wait_recv()
    attn = jnp.concatenate([part_in[s] + part_in[4 + s] for s in range(GROUPS)], axis=0)
    x1 = (x_ref[...].astype(F32) + attn).astype(BF16).astype(F32)
    for k in range(8):
        x1_ref[k] = x1[2 * k : 2 * k + 2, :]
    normed = rms_norm(x1, g_ref[...].astype(F32))
    up = jnp.dot(normed, wu[...], preferred_element_type=F32)
    act = jax.nn.gelu(up, approximate=True).astype(BF16)
    down = jnp.dot(act, wd[...], preferred_element_type=F32)
    for k in range(8):
        mlp_out[k] = down[2 * k : 2 * k + 2, :]

    def mlp_copy(j, sending):
        t, s = peer(*others[j])
        ft, fs = source(*others[j])
        slot = me if sending else ft * 4 + fs
        return remote(mlp_out.at[t * 4 + s], mlp_in.at[slot], mlp_s.at[j], mlp_r.at[j], t, s)

    for j in range(7):
        mlp_copy(j, True).start()
    mlp_in[me] = mlp_out[me]
    for j in range(7):
        mlp_copy(j, True).wait_send()
        mlp_copy(j, False).wait_recv()
    tot = mlp_in[0]
    for k in range(1, 8):
        tot = tot + mlp_in[k]
    fin_out[...] = (x1_ref[me] + tot).astype(BF16).astype(F32)

    def fin_copy(j, sending):
        t, s = peer(*others[j])
        ft, fs = source(*others[j])
        slot = me if sending else ft * 4 + fs
        return remote(fin_out, fin_in.at[slot], fin_s.at[j], fin_r.at[j], t, s)

    for j in range(7):
        fin_copy(j, True).start()
    fin_in[me] = fin_out[...]
    for j in range(7):
        fin_copy(j, True).wait_send()
        fin_copy(j, False).wait_recv()
    out_ref[...] = jnp.concatenate([fin_in[k] for k in range(8)], axis=0).astype(BF16)


def solution(mesh):
    spec_rows = P('dp', None)
    spec_cache = P('dp', 'sp', 'tp', None)
    in_specs = (spec_rows, spec_cache, spec_cache, P('dp'), P('sp', 'tp', None), P('tp', None), P('tp', None), P(None), P(None, 'tp', None), P(None, 'tp', None), P(None, 'tp', None), P('tp', None, None), P(None), P(None, 'tp'), P('tp', None))
    out_specs = spec_rows
    vm = pl.BlockSpec(memory_space=VMEM)
    hbm = pl.BlockSpec(memory_space=pl.ANY)
    smem = pl.BlockSpec(memory_space=pltpu.SMEM)
    dma = pltpu.SemaphoreType.DMA

    def layer_step(hidden, k_cache, v_cache, lengths, rel_table, u_bias, w_bias, g_attn, w_query, w_key, w_value, w_out, g_mlp, w_up, w_down):
        heads_first = lambda w: jnp.transpose(w, (1, 0, 2))
        qr, rolled, aux = pl.pallas_call(
            front_kernel,
            out_shape=(
                jax.ShapeDtypeStruct((128, HEADS * HEAD), BF16),
                jax.ShapeDtypeStruct((TILES, ROWS, 128), F32),
                jax.ShapeDtypeStruct((3, ROWS, 128), F32),
            ),
            in_specs=[smem, vm, vm, vm, vm, hbm, hbm, hbm, hbm],
            out_specs=(vm, vm, vm),
            scratch_shapes=[
                VMEM((HEADS, D, HEAD), BF16), VMEM((HEADS, D, HEAD), BF16), VMEM((HEADS, D, HEAD), BF16),
                VMEM((HEADS, BLK, HEAD), BF16), VMEM((128, HEADS * HEAD), F32), VMEM((TILES, ROWS, 128), F32),
                dma((4, HEADS)),
            ],
            compiler_params=pltpu.CompilerParams(vmem_limit_bytes=60 * 2**20),
            name="front",
        )(lengths, hidden, g_attn.reshape(1, D), u_bias, w_bias, heads_first(w_query), heads_first(w_key), heads_first(w_value), heads_first(rel_table))
        return pl.pallas_call(
            main_kernel,
            out_shape=jax.ShapeDtypeStruct((BATCH, D), BF16),
            in_specs=[hbm, hbm, vm, vm, vm, vm, vm, hbm, hbm, hbm],
            out_specs=vm,
            scratch_shapes=[
                VMEM((RING, HEADS, BLK, HEAD), BF16),
                VMEM((HEADS * HEAD, D), BF16), VMEM((D, HID), BF16), VMEM((HID, D), BF16),
                VMEM((BLK, 128), F32), VMEM((TILES, ROWS, 128), F32),
                VMEM((TILES, ROWS, 128), F32), VMEM((TILES, ROWS, 128), F32), VMEM((TILES, ROWS, 128), F32),
                VMEM((ROWS, 128), F32), VMEM((3, ROWS, 128), F32), VMEM((ROWS, 128), F32),
                VMEM((GROUPS, GROWS, 128), F32), VMEM((4, GROWS, 128), F32),
                VMEM((PER, D), F32), VMEM((8, PER, D), F32), VMEM((8, 2, D), F32),
                VMEM((8, 2, D), F32), VMEM((8, 2, D), F32), VMEM((2, D), F32), VMEM((8, 2, D), F32),
                dma((RING,)), dma((3,)), dma((4,)), dma((4,)), dma((4,)), dma((4,)), dma((3,)), dma((3,)), dma((3,)), dma((3,)),
                dma((7,)), dma((7,)), dma((7,)), dma((7,)), dma((7,)), dma((7,)),
            ],
            compiler_params=pltpu.CompilerParams(vmem_limit_bytes=60 * 2**20, collective_id=0, has_side_effects=True),
            name="main",
        )(
            jnp.transpose(k_cache, (0, 2, 1, 3)), jnp.transpose(v_cache, (0, 2, 1, 3)), qr, rolled, aux,
            hidden, g_mlp.reshape(1, D), w_out.reshape(HEADS * HEAD, D), w_up, w_down,
        )

    return jax.shard_map(layer_step, mesh=mesh, in_specs=in_specs, out_specs=out_specs, check_vma=False)
```

time: 181 us -> 66.7 us (0.37)
  Pallas kernels: 0 us -> 62.4 us
  matrix products: 59.1 us -> 0 us
  local copies, waits for them, and re-layouts: 55.2 us -> 3.99 us
  waiting for transfers between devices: 34.2 us -> 0 us
  between operations: 13.3 us -> 0.02 us
  blocking collectives: 8.91 us -> 0 us
  other arithmetic: 7.89 us -> 0 us
    pallas_call x0 -> x2, Pallas kernels: none -> 62.4 us  [the longest x1 54.1 us: layer_step(): pl.pallas_call(main_kernel, out_shape=jax.ShapeDtypeStruct((BATCH, D), BF...]
    dot_general x8 -> x0, matrix products: 59.1 us -> none  [the longest x1 21.4 us: layer_step(): jnp.einsum('bhd,bshd->bhs', q_content, k_updated, preferred_element_type=...]
    gather x64 -> x0, local copies, waits for them, and re-layouts: 49.1 us -> none
    psum x2 -> x0, waiting for transfers between devices: 31.7 us -> none  [the longest x1 16.1 us: layer_step(): attn_out = lax.psum(attn_part, 'tp')]
    all_gather x1 -> x0, blocking collectives: 8.91 us -> none  [layer_step(): gathered = lax.all_gather(packed, 'sp', axis=0)]
    convert_element_type x7 -> x0, other arithmetic: 4.48 us -> none  [the longest x1 1.52 us: layer_step(): (resid_mid.astype(jnp.float32) + down_proj).astype(jnp.bfloat16)]
    pad x1 -> x0, local copies, waits for them, and re-layouts: 4.15 us -> none  [distance_to_position(): padded = jnp.pad(by_distance, ((0, 0), (0, 0), (width, 0)))]
    reshape x0 -> x2, local copies, waits for them, and re-layouts: none -> 2.56 us  [the longest x1 1.28 us: layer_step(): g_attn.reshape(1, D)]
  transfers between devices with their start and end apart: 3 -> 0, of which waited for: 3 -> 0; matrix products, arithmetic and copies ran while one was open for 14% -> 0% of each run, Pallas kernels for 0% -> 0%
where the time goes in v1:
time: 66.7 us; the launch traced here: 66.4 us
  Pallas kernels  62.4 us (94%)
  local copies, waits for them, and re-layouts  3.99 us (6%)
    pallas_call x1, Pallas kernels, layer_step(): pl.pallas_call(main_kernel, out_shape=jax.ShapeDtypeStruct((BATCH, D), BF...  54.1 us
    pallas_call x1, Pallas kernels, layer_step(): pl.pallas_call(front_kernel, out_shape=(jax.ShapeDtypeStruct((128, HEADS...  8.28 us
    unnamed x1, local copies, waits for them, and re-layouts  1.42 us

profile of v1, /device:TPU:0, one launch (start us, length us, event | category | flops | bytes accessed | tf_op | source)
XLA Modules:
  0.0 66.4 jit_solution(2452246469976610712)
XLA Ops:
  0.0 1.3 %reshape.9.g_ref = bf16[1,1536]{1,0:T(2,128)(2,1)} reshape(bf16[1536]{0:T(1024)(128)(2,1)} %param.22) | data formatting | bytes 6144 | tf_op jit(solution)/shard_map/reshape | solution.py:378
  1.3 1.3 %reshape.10.g_ref = bf16[1,1536]{1,0:T(2,128)(2,1)} reshape(bf16[1536]{0:T(1024)(128)(2,1)} %param.27) | data formatting | bytes 6144 | tf_op jit(solution)/shard_map/reshape | solution.py:400
  2.6 8.3 %front.1 = (bf16[128,768]{1,0:T(8,128)(2,1)}, f32[16,96,128]{2,1,0:T(8,128)}, f32[3,96,128]{2,1,0:T(8,128)}) custom-call(s32[16]{0:T(128)} %len_ref.1, bf16[16,1536]{1,0:T(8,128)(2,1)} %x_ref.3, bf16[1,1536]{1,0:T(2,128)(2,1)} %reshape.9.g_ref, bf16[6,128]{1,0:T(8,128)(2,1)} %u_ref.1, bf16[6,128]{1,0:T(8,128)(2,1)} %wb_ref.1, ...), custom_call_target="tpu_custom_call" | custom-call | tf_op jit(solution)/shard_map/front/pallas_call | solution.py:362
  10.9 54.1 %main.1 = bf16[16,1536]{1,0:T(8,128)(2,1)} custom-call(bf16[16,6,2048,128]{3,2,1,0:T(8,128)(2,1)} %bitcast.7, bf16[16,6,2048,128]{3,2,1,0:T(8,128)(2,1)} %bitcast.8, bf16[128,768]{1,0:T(8,128)(2,1)} %get-tuple-element.8.qr_ref, f32[16,96,128]{2,1,0:T(8,128)} %get-tuple-element.9.rolled, f32[3,96,128]{2,1,0:T(8,128)} %get-tuple-element.10.aux, ...), custom_call_target="tpu_custom_call" | custom-call | tf_op jit(solution)/shard_map/main/pallas_call | solution.py:379
  65.0 1.4 %copy.17 = bf16[16,1536]{1,0:T(8,128)(2,1)} copy(bf16[16,1536]{1,0:T(8,128)(2,1)} %main.1) | data formatting | bytes 98304

commit v2 on v0

v2 whole, which is shorter than its diff:
```python
import functools

import jax
import jax.numpy as jnp
from jax import lax
from jax.experimental import pallas as pl
from jax.experimental.pallas import tpu as pltpu
from jax.sharding import PartitionSpec as P

EPS = 1e-6
MASKED = -1e30
MESH = pl.DeviceIdType.MESH
F32 = jnp.float32
BF16 = jnp.bfloat16
VMEM = pltpu.VMEM
NT = (((1,), (1,)), ((), ()))

BATCH, HEADS, HEAD, BLK, D = 16, 6, 128, 2048, 1536
TILES = BLK // 128
GROUPS, PER = 4, 4
GROWS = HEADS * PER
ROWS = GROUPS * GROWS
RING = 9
HID = 768


def rms_norm(wide, gain):
    mean_sq = jnp.mean(wide * wide, axis=-1, keepdims=True)
    return (wide * lax.rsqrt(mean_sq + EPS) * gain).astype(BF16)


def fused_kernel(len_ref, x_hbm, g1_hbm, g2_hbm, u_hbm, wb_hbm, wq_hbm, wk_hbm, wv_hbm, rel_hbm, k_hbm, v_hbm, wo_hbm, wu_hbm, wd_hbm,
                 out_ref,
                 xb, g1, g2, ub, wbb, wq, wk, wv, rel, qf, qc_ref, raw, new_score, new_value, new_prob,
                 ring, wo, wu, wd, score, rolled, from_pair, to_far, from_far, probs, stat_out, stat_in, ctx, ctx_in,
                 part_out, part_in, x1_ref, mlp_in,
                 small_sem, in_sem, ring_sem, w_sem, pair_s, pair_r, far_s, far_r, stat_s, stat_r, ctx_s, ctx_r,
                 part_s, part_r, mlp_s, mlp_r):
    tp, sp = lax.axis_index("tp"), lax.axis_index("sp")
    me = tp * 4 + sp
    odd = lax.rem(sp, 2)
    pair = sp + 1 - 2 * odd

    small = [pltpu.make_async_copy(a, b, small_sem.at[i]) for i, (a, b) in enumerate(
        ((x_hbm, xb), (g1_hbm, g1), (g2_hbm, g2), (u_hbm, ub), (wb_hbm, wbb)))]

    def head_copy(j, h):
        a, b = ((wq_hbm, wq), (rel_hbm, rel), (wk_hbm, wk), (wv_hbm, wv))[j]
        return pltpu.make_async_copy(a.at[h], b.at[h], in_sem.at[j, h])

    weights = (
        pltpu.make_async_copy(wo_hbm, wo, w_sem.at[0]),
        pltpu.make_async_copy(wu_hbm.at[:, pl.ds(pl.multiple_of(sp * HID, 128), HID)], wu, w_sem.at[1]),
        pltpu.make_async_copy(wd_hbm.at[pl.ds(pl.multiple_of(sp * HID, 128), HID), :], wd, w_sem.at[2]),
    )

    def load(step, slot):
        @pl.when(step < BATCH)
        def _():
            pltpu.make_async_copy(k_hbm.at[step], ring.at[slot], ring_sem.at[slot]).start()

        @pl.when(jnp.logical_and(step >= BATCH, step < 2 * BATCH))
        def _():
            pltpu.make_async_copy(v_hbm.at[step - BATCH], ring.at[slot], ring_sem.at[slot]).start()

    for c in small:
        c.start()
    for j in range(2):
        for h in range(HEADS):
            head_copy(j, h).start()
    for i in range(RING):
        pltpu.make_async_copy(k_hbm.at[i], ring.at[i], ring_sem.at[i]).start()

    others = [(dt, ds) for dt in range(2) for ds in range(4) if (dt, ds) != (0, 0)]

    def peer(dt, ds):
        return lax.rem(tp + dt, 2), lax.rem(sp + ds, 4)

    def source(dt, ds):
        return lax.rem(tp + 2 - dt, 2), lax.rem(sp + 4 - ds, 4)

    barrier = pltpu.get_barrier_semaphore()
    for dt, ds in others:
        t, s = peer(dt, ds)
        pl.semaphore_signal(barrier, inc=1, device_id={"tp": t, "sp": s}, device_id_type=MESH)

    def remote(src, dst, send, recv, t, s):
        return pltpu.make_async_remote_copy(
            src_ref=src, dst_ref=dst, send_sem=send, recv_sem=recv, device_id={"tp": t, "sp": s}, device_id_type=MESH
        )

    def rows(g):
        return pl.ds(pl.multiple_of(g * GROWS, 8), GROWS)

    def pair_copy(g):
        return remote(rolled.at[:, rows(g), :], from_pair.at[:, rows(g), :], pair_s.at[g], pair_r.at[g], tp, pair)

    def far_copy(g):
        return remote(to_far.at[:, rows(g), :], from_far.at[:, rows(g), :], far_s.at[g], far_r.at[g], tp, 3 - sp)

    def stat_copy(g, ds):
        t, s = peer(0, ds)
        return remote(stat_out.at[rows(g), :], stat_in.at[ds - 1, rows(g), :], stat_s.at[g, ds - 1], stat_r.at[g, ds - 1], t, s)

    def ctx_copy(g, ds, sending):
        t, s = peer(0, ds)
        _, fs = source(0, ds)
        slot = sp if sending else fs
        return remote(ctx_in.at[slot, rows(g), :], ctx_in.at[slot, rows(g), :], ctx_s.at[g, ds - 1], ctx_r.at[g, ds - 1], t, s)

    def part_copy(g):
        return remote(part_out.at[g], part_in.at[g], part_s.at[g], part_r.at[g], 1 - tp, sp)

    def mlp_copy(g, j, sending):
        t, s = peer(*others[j])
        ft, fs = source(*others[j])
        slot = me if sending else ft * 4 + fs
        return remote(mlp_in.at[g, slot], mlp_in.at[g, slot], mlp_s.at[g, j], mlp_r.at[g, j], t, s)

    for c in small:
        c.wait()
    x = xb[...].astype(F32)
    for g in range(GROUPS):
        x1_ref[g] = x[PER * g : PER * g + PER, :]
    normed = rms_norm(x, g1[...].astype(F32).reshape(1, D))
    qf[...] = jnp.zeros_like(qf)
    for h in range(HEADS):
        head_copy(0, h).wait()
        q = jnp.dot(normed, wq[h], preferred_element_type=F32).astype(BF16).astype(F32)
        qc = (q + ub[h : h + 1, :].astype(F32)).astype(BF16).astype(F32)
        qp = (q + wbb[h : h + 1, :].astype(F32)).astype(BF16)
        qc_ref[h] = qc
        qf[h, pl.ds(h, BATCH, stride=8), :] = qc
        head_copy(1, h).wait()
        by_dist = lax.dot_general(qp, rel[h], NT, preferred_element_type=F32)
        for c in range(TILES):
            for s in range(GROUPS):
                row = s * GROWS + h * PER
                raw[c, row : row + PER, :] = by_dist[s * PER : s * PER + PER, c * 128 : c * 128 + 128]

    def lengths_of(group, count):
        seq = lax.rem(lax.broadcasted_iota(jnp.int32, (count, 128), 0), PER)
        out = jnp.zeros((count, 128), jnp.int32) + len_ref[PER * group]
        for i in range(1, PER):
            out = jnp.where(seq == i, len_ref[PER * group + i], out)
        return out

    lane8 = lax.broadcasted_iota(jnp.int32, (8, 128), 1)

    def roll(piece):
        r = lax.rem(lengths_of(lax.div(piece, GROWS // 8), 8), BLK)
        big, small_r = lax.div(r, 128), lax.rem(r, 128)
        sl = pl.ds(pl.multiple_of(piece * 8, 8), 8)
        idx = lax.rem(small_r - lane8 + 128, 128)
        tiles = [jnp.take_along_axis(raw[(TILES - c) % TILES, sl, :], idx, axis=1) for c in range(TILES)]
        for k in range(4):
            bit = lax.rem(lax.div(big, 1 << k), 2) == 1
            tiles = [jnp.where(bit, tiles[(c - (1 << k)) % TILES], tiles[c]) for c in range(TILES)]
        low = lane8 <= small_r
        for c in range(TILES):
            rolled[c, sl, :] = jnp.where(low, tiles[c], tiles[(c + 1) % TILES])

    def content(b):
        slot = lax.rem(b, RING)
        pltpu.make_async_copy(k_hbm.at[b], ring.at[slot], ring_sem.at[slot]).wait()
        sl = pl.ds(pl.multiple_of(b * 8, 8), 8)
        total = None
        for p in range(HEADS // 2):
            keys = jnp.concatenate([ring[slot, 2 * p], ring[slot, 2 * p + 1]], axis=1)
            query = jnp.concatenate([qf[2 * p, sl, :], qf[2 * p + 1, sl, :]], axis=1).astype(BF16)
            dots = lax.dot_general(query, keys, NT, preferred_element_type=F32)
            total = dots if total is None else total + dots
        first = lax.div(b, PER) * GROWS + lax.rem(b, PER)
        for c in range(TILES):
            score[c, pl.ds(first, HEADS, stride=PER), :] = total[:HEADS, c * 128 : c * 128 + 128]
        return slot

    lane24 = lax.broadcasted_iota(jnp.int32, (GROWS, 128), 1)

    def merge(g):
        pair_copy(g).wait()
        n = lengths_of(g, GROWS)
        r = lax.rem(n, BLK)
        last = lax.div(n, BLK) == 3
        for c in range(TILES):
            mine = jnp.logical_or(jnp.logical_and(last, lane24 + 128 * c <= r), odd == 0)
            to_far[c, rows(g), :] = jnp.where(mine, rolled[c, rows(g), :], from_pair[c, rows(g), :])

    def k_tail(b, slot):
        load(b + RING, slot)
        g, i = lax.div(b, 3), lax.rem(b, 3)

        @pl.when(jnp.logical_and(i == 2, g < GROUPS))
        def _():
            pair_copy(g).start()

        @pl.when(jnp.logical_and(i == 2, g >= 1))
        def _():
            merge(g - 1)

        @pl.when(jnp.logical_and(i == 0, g >= 2))
        def _():
            far_copy(g - 2).start()

    pl.semaphore_wait(barrier, 7)

    def k_early(b, _):
        slot = content(b)
        roll(b)
        k_tail(b, slot)

        @pl.when(b == 2)
        def _():
            for j in (2, 3):
                for h in range(HEADS):
                    head_copy(j, h).start()

        @pl.when(b == 8)
        def _():
            for w in weights:
                w.start()

        return 0

    def k_late(b, _):
        slot = content(b)
        k_tail(b, slot)
        return 0

    lax.fori_loop(0, 12, k_early, 0)
    for h in range(HEADS):
        head_copy(2, h).wait()
        kn = jnp.dot(normed, wk[h], preferred_element_type=F32).astype(BF16).astype(F32)
        head_copy(3, h).wait()
        vn = jnp.dot(normed, wv[h], preferred_element_type=F32).astype(BF16).astype(F32)
        sn = jnp.broadcast_to(jnp.sum(qc_ref[h] * kn, axis=1, keepdims=True), (BATCH, 128))
        for s in range(GROUPS):
            row = s * GROWS + h * PER
            new_score[row : row + PER, :] = sn[s * PER : s * PER + PER, :]
            new_value[row : row + PER, :] = vn[s * PER : s * PER + PER, :]
    lax.fori_loop(12, BATCH, k_late, 0)

    lane6 = lax.broadcasted_iota(jnp.int32, (HEADS, 128), 1)
    head_row = lax.broadcasted_iota(jnp.int32, (HEADS, 128), 0)

    def softmax(b):
        sl = pl.ds(lax.div(b, PER) * GROWS + lax.rem(b, PER), HEADS, stride=PER)
        n = len_ref[b]
        r = lax.rem(n, BLK)
        block = lax.div(n, BLK)
        here = n - sp * BLK
        new = new_score[sl, :]
        own_a, pair_a = block - sp == sp, block - sp == pair
        own_b, pair_b = block - sp - 1 == sp, block - sp - 1 == pair
        sc = []
        for c in range(TILES):
            pos = lane6 + 128 * c
            own, near, far = rolled[c, sl, :], from_pair[c, sl, :], from_far[c, sl, :]
            rel_a = jnp.where(own_a, own, jnp.where(pair_a, near, far))
            rel_b = jnp.where(own_b, own, jnp.where(pair_b, near, far))
            rel_c = jnp.where(pos <= r, rel_a, rel_b)
            con = jnp.where(pos == here, new, score[c, sl, :])
            sc.append(jnp.where(pos <= here, (con + rel_c) * (HEAD**-0.5), MASKED))
        top = functools.reduce(jnp.maximum, sc)
        top = jnp.max(top, axis=1, keepdims=True)
        total = jnp.zeros((HEADS, 128), F32)
        at_new = jnp.zeros((HEADS, 128), F32)
        slot = lax.rem(b, 3)
        for c in range(TILES):
            pos = lane6 + 128 * c
            w = jnp.where(pos <= here, jnp.exp(sc[c] - top), 0.0)
            total = total + w
            at_new = at_new + jnp.where(pos == here, w.astype(BF16).astype(F32), 0.0)
            probs[slot, :, c * 128 : c * 128 + 128] = jnp.where(pos == here, 0.0, w)
        total = jnp.sum(total, axis=1, keepdims=True)
        at_new = jnp.sum(at_new, axis=1, keepdims=True)
        stat_out[sl, :] = jnp.where(lane6 < 64, top, total)
        new_prob[sl, :] = jnp.broadcast_to(at_new, (HEADS, 128))

    def attend(b):
        slot = lax.rem(b + BATCH, RING)
        pltpu.make_async_copy(v_hbm.at[b], ring.at[slot], ring_sem.at[slot]).wait()
        pb = probs[lax.rem(b, 3)].astype(BF16)
        out = jnp.zeros((HEADS, 128), F32)
        for p in range(HEADS // 2):
            values = jnp.concatenate([ring[slot, 2 * p], ring[slot, 2 * p + 1]], axis=1)
            dots = jnp.dot(pb, values, preferred_element_type=F32)
            out = jnp.where(head_row == 2 * p, dots[:, :128], jnp.where(head_row == 2 * p + 1, dots[:, 128:], out))
        ctx[pl.ds(lax.div(b, PER) * GROWS + lax.rem(b, PER), HEADS, stride=PER), :] = out
        return slot

    def send_stats(g):
        for ds in range(1, 4):
            stat_copy(g, ds).start()

    def send_ctx(g):
        for ds in range(1, 4):
            stat_copy(g, ds).wait()
        mine = stat_out[rows(g), :]
        top, total = mine[:, :1], mine[:, 64:65]
        all_top = top
        for ds in range(3):
            all_top = jnp.maximum(all_top, stat_in[ds, rows(g), :][:, :1])
        all_total = total * jnp.exp(top - all_top)
        for ds in range(3):
            got = stat_in[ds, rows(g), :]
            all_total = all_total + got[:, 64:65] * jnp.exp(got[:, :1] - all_top)
        scale = jnp.exp(top - all_top) / all_total
        ctx_in[sp, rows(g), :] = (ctx[rows(g), :] + new_prob[rows(g), :] * new_value[rows(g), :]) * scale
        for ds in range(1, 4):
            ctx_copy(g, ds, True).start()

    def project(g):
        for ds in range(1, 4):
            ctx_copy(g, ds, True).wait_send()
            ctx_copy(g, ds, False).wait_recv()
        whole = (ctx_in[0, rows(g), :] + ctx_in[1, rows(g), :]) + (ctx_in[2, rows(g), :] + ctx_in[3, rows(g), :])
        lhs = jnp.concatenate([whole[h * PER : h * PER + PER, :] for h in range(HEADS)], axis=1).astype(BF16)
        part_out[g] = jnp.dot(lhs, wo[...], preferred_element_type=F32)
        part_copy(g).start()

    def mlp(g):
        part_copy(g).wait()
        x1 = (x1_ref[g] + (part_out[g] + part_in[g])).astype(BF16).astype(F32)
        x1_ref[g] = x1
        up = jnp.dot(rms_norm(x1, g2[...].astype(F32).reshape(1, D)), wu[...], preferred_element_type=F32)
        act = jax.nn.gelu(up, approximate=True).astype(BF16)
        mlp_in[g, me] = jnp.dot(act, wd[...], preferred_element_type=F32)
        for j in range(7):
            mlp_copy(g, j, True).start()

    def finish(g):
        for j in range(7):
            mlp_copy(g, j, True).wait_send()
            mlp_copy(g, j, False).wait_recv()
        tot = mlp_in[g, 0]
        for k in range(1, 8):
            tot = tot + mlp_in[g, k]
        return x1_ref[g] + tot

    far_copy(0).wait()
    softmax(0)
    softmax(1)

    def v_step(b, _):
        g, i = lax.div(b, PER), lax.rem(b, PER)

        @pl.when(jnp.logical_and(i == 2, g < GROUPS - 1))
        def _():
            far_copy(g + 1).wait()

        slot = attend(b)
        softmax(b + 2)
        load(b + BATCH + RING, slot)

        @pl.when(b == 3)
        def _():
            for w in weights:
                w.wait()

        @pl.when(i == 1)
        def _():
            send_stats(g)

        @pl.when(i == 3)
        def _():
            send_ctx(g)

        @pl.when(jnp.logical_and(i == 2, g >= 1))
        def _():
            project(g - 1)

        @pl.when(jnp.logical_and(i == 1, g >= 2))
        def _():
            mlp(g - 2)

        return 0

    lax.fori_loop(0, BATCH - 2, v_step, 0)
    attend(jnp.int32(BATCH - 2))
    project(GROUPS - 2)
    attend(jnp.int32(BATCH - 1))
    send_ctx(GROUPS - 1)
    mlp(GROUPS - 2)
    project(GROUPS - 1)
    done = [finish(0), finish(1)]
    mlp(GROUPS - 1)
    done = done + [finish(2), finish(3)]
    out_ref[...] = jnp.concatenate(done, axis=0).astype(BF16)


def solution(mesh):
    spec_rows = P('dp', None)
    spec_cache = P('dp', 'sp', 'tp', None)
    in_specs = (spec_rows, spec_cache, spec_cache, P('dp'), P('sp', 'tp', None), P('tp', None), P('tp', None), P(None), P(None, 'tp', None), P(None, 'tp', None), P(None, 'tp', None), P('tp', None, None), P(None), P(None, 'tp'), P('tp', None))
    out_specs = spec_rows
    vm = pl.BlockSpec(memory_space=VMEM)
    hbm = pl.BlockSpec(memory_space=pl.ANY)
    smem = pl.BlockSpec(memory_space=pltpu.SMEM)
    dma = pltpu.SemaphoreType.DMA
    head_weight = VMEM((HEADS, D, HEAD), BF16)
    tiles = VMEM((TILES, ROWS, 128), F32)
    by_row = VMEM((ROWS, 128), F32)

    def layer_step(hidden, k_cache, v_cache, lengths, rel_table, u_bias, w_bias, g_attn, w_query, w_key, w_value, w_out, g_mlp, w_up, w_down):
        heads_first = lambda w: jnp.transpose(w, (1, 0, 2))
        return pl.pallas_call(
            fused_kernel,
            out_shape=jax.ShapeDtypeStruct((BATCH, D), BF16),
            in_specs=[smem] + [hbm] * 14,
            out_specs=vm,
            scratch_shapes=[
                VMEM((BATCH, D), BF16), VMEM((D,), BF16), VMEM((D,), BF16), VMEM((HEADS, HEAD), BF16), VMEM((HEADS, HEAD), BF16),
                head_weight, head_weight, head_weight, VMEM((HEADS, BLK, HEAD), BF16),
                VMEM((HEADS, 128, 128), F32), VMEM((HEADS, BATCH, 128), F32), tiles, by_row, by_row, by_row,
                VMEM((RING, HEADS, BLK, HEAD), BF16), VMEM((HEADS * HEAD, D), BF16), VMEM((D, HID), BF16), VMEM((HID, D), BF16),
                tiles, tiles, tiles, tiles, tiles, VMEM((3, HEADS, BLK), F32),
                by_row, VMEM((3, ROWS, 128), F32), by_row, VMEM((4, ROWS, 128), F32),
                VMEM((GROUPS, PER, D), F32), VMEM((GROUPS, PER, D), F32), VMEM((GROUPS, PER, D), F32), VMEM((GROUPS, 8, PER, D), F32),
                dma((5,)), dma((4, HEADS)), dma((RING,)), dma((3,)), dma((4,)), dma((4,)), dma((4,)), dma((4,)),
                dma((4, 3)), dma((4, 3)), dma((4, 3)), dma((4, 3)), dma((4,)), dma((4,)), dma((4, 7)), dma((4, 7)),
            ],
            compiler_params=pltpu.CompilerParams(vmem_limit_bytes=63 * 2**20, collective_id=0, has_side_effects=True),
            name="layer",
        )(
            lengths, hidden, g_attn, g_mlp, u_bias, w_bias,
            heads_first(w_query), heads_first(w_key), heads_first(w_value), heads_first(rel_table),
            jnp.transpose(k_cache, (0, 2, 1, 3)), jnp.transpose(v_cache, (0, 2, 1, 3)),
            w_out.reshape(HEADS * HEAD, D), w_up, w_down,
        )

    return jax.shard_map(layer_step, mesh=mesh, in_specs=in_specs, out_specs=out_specs, check_vma=False)
```

time: 181 us -> 70.9 us (0.39)
  Pallas kernels: 0 us -> 69.3 us
  matrix products: 59.1 us -> 0 us
  local copies, waits for them, and re-layouts: 55.2 us -> 1.42 us
  waiting for transfers between devices: 34.2 us -> 0 us
  between operations: 13.3 us -> 0.01 us
  blocking collectives: 8.91 us -> 0 us
  other arithmetic: 7.89 us -> 0 us
    pallas_call x0 -> x1, Pallas kernels: none -> 69.3 us  [layer_step(): pl.pallas_call(fused_kernel, out_shape=jax.ShapeDtypeStruct((BATCH, D), B...]
    dot_general x8 -> x0, matrix products: 59.1 us -> none  [the longest x1 21.4 us: layer_step(): jnp.einsum('bhd,bshd->bhs', q_content, k_updated, preferred_element_type=...]
    gather x64 -> x0, local copies, waits for them, and re-layouts: 49.1 us -> none
    psum x2 -> x0, waiting for transfers between devices: 31.7 us -> none  [the longest x1 16.1 us: layer_step(): attn_out = lax.psum(attn_part, 'tp')]
    all_gather x1 -> x0, blocking collectives: 8.91 us -> none  [layer_step(): gathered = lax.all_gather(packed, 'sp', axis=0)]
    convert_element_type x7 -> x0, other arithmetic: 4.48 us -> none  [the longest x1 1.52 us: layer_step(): (resid_mid.astype(jnp.float32) + down_proj).astype(jnp.bfloat16)]
    pad x1 -> x0, local copies, waits for them, and re-layouts: 4.15 us -> none  [distance_to_position(): padded = jnp.pad(by_distance, ((0, 0), (0, 0), (width, 0)))]
    all_gather x1 -> x0, waiting for transfers between devices: 2.42 us -> none  [layer_step(): rel_all = lax.all_gather(rel_local, 'sp', axis=2, tiled=True)]
  transfers between devices with their start and end apart: 3 -> 0, of which waited for: 3 -> 0; matrix products, arithmetic and copies ran while one was open for 14% -> 0% of each run, Pallas kernels for 0% -> 0%
where the time goes in v2:
time: 70.9 us; the launch traced here: 70.7 us
  Pallas kernels  69.3 us (98%)
  local copies, waits for them, and re-layouts  1.42 us (2%)
    pallas_call x1, Pallas kernels, layer_step(): pl.pallas_call(fused_kernel, out_shape=jax.ShapeDtypeStruct((BATCH, D), B...  69.3 us
    unnamed x1, local copies, waits for them, and re-layouts  1.42 us

profile of v2, /device:TPU:0, one launch (start us, length us, event | category | flops | bytes accessed | tf_op | source)
XLA Modules:
  0.0 70.7 jit_solution(17687322515145512437)
XLA Ops:
  0.0 69.3 %layer.1 = bf16[16,1536]{1,0:T(8,128)(2,1)} custom-call(s32[16]{0:T(128)} %len_ref.1, bf16[16,1536]{1,0:T(8,128)(2,1)} %x_hbm.1, bf16[1536]{0:T(1024)(128)(2,1)} %g1_hbm.1, bf16[1536]{0:T(1024)(128)(2,1)} %g2_hbm.1, bf16[6,128]{1,0:T(8,128)(2,1)} %u_hbm.1, bf16[6,128]{1,0:T(8,128)(2,1)} %wb_hbm.1, bf16[6,1536,128]{2,1,0:T(8,128)(2,1)} %bitcast.10, ...), custom_call_target="tpu_custom_call" | custom-call | tf_op jit(solution)/shard_map/layer/pallas_call | solution.py:407
  69.3 1.4 %copy.17 = bf16[16,1536]{1,0:T(8,128)(2,1)} copy(bf16[16,1536]{1,0:T(8,128)(2,1)} %layer.1) | data formatting | bytes 98304

commit v3 on v2

--- a/solution.py
+++ b/solution.py
@@ -20,7 +20,8 @@
 GROUPS, PER = 4, 4
 GROWS = HEADS * PER
 ROWS = GROUPS * GROWS
-RING = 9
+RING = 8
+FIRST = 3
 HID = 768
 
 
@@ -68,7 +69,7 @@
     for j in range(2):
         for h in range(HEADS):
             head_copy(j, h).start()
-    for i in range(RING):
+    for i in range(FIRST):
         pltpu.make_async_copy(k_hbm.at[i], ring.at[i], ring_sem.at[i]).start()
 
     others = [(dt, ds) for dt in range(2) for ds in range(4) if (dt, ds) != (0, 0)]
@@ -95,8 +96,8 @@
     def pair_copy(g):
         return remote(rolled.at[:, rows(g), :], from_pair.at[:, rows(g), :], pair_s.at[g], pair_r.at[g], tp, pair)
 
-    def far_copy(g):
-        return remote(to_far.at[:, rows(g), :], from_far.at[:, rows(g), :], far_s.at[g], far_r.at[g], tp, 3 - sp)
+    def far_copy(g, src=None):
+        return remote((to_far if src is None else src).at[:, rows(g), :], from_far.at[:, rows(g), :], far_s.at[g], far_r.at[g], tp, 3 - sp)
 
     def stat_copy(g, ds):
         t, s = peer(0, ds)
@@ -186,48 +187,62 @@
             mine = jnp.logical_or(jnp.logical_and(last, lane24 + 128 * c <= r), odd == 0)
             to_far[c, rows(g), :] = jnp.where(mine, rolled[c, rows(g), :], from_pair[c, rows(g), :])
 
-    def k_tail(b, slot):
-        load(b + RING, slot)
-        g, i = lax.div(b, 3), lax.rem(b, 3)
-
-        @pl.when(jnp.logical_and(i == 2, g < GROUPS))
-        def _():
-            pair_copy(g).start()
-
-        @pl.when(jnp.logical_and(i == 2, g >= 1))
-        def _():
-            merge(g - 1)
-
-        @pl.when(jnp.logical_and(i == 0, g >= 2))
-        def _():
-            far_copy(g - 2).start()
+    def refill(b, slot):
+        @pl.when(b <= RING - FIRST - 1)
+        def _():
+            for k in range(2):
+                nxt = FIRST + 2 * b + k
+                load(nxt, lax.rem(nxt, RING))
+
+        @pl.when(b > RING - FIRST - 1)
+        def _():
+            load(b + RING, slot)
 
     pl.semaphore_wait(barrier, 7)
 
-    def k_early(b, _):
+    def send(g):
+        pair_copy(g).start()
+
+        @pl.when(odd == 0)
+        def _():
+            far_copy(g, rolled).start()
+
+    for b in range(3):
+        slot = content(jnp.int32(b))
+        for k in range(4):
+            roll(4 * b + k)
+        refill(jnp.int32(b), slot)
+        send(b)
+    send(3)
+
+    def k_mid(b, _):
         slot = content(b)
-        roll(b)
-        k_tail(b, slot)
-
-        @pl.when(b == 2)
+        refill(b, slot)
+
+        @pl.when(odd == 1)
+        def _():
+            @pl.when(b < 3 + GROUPS)
+            def _():
+                merge(b - 3)
+
+            @pl.when(jnp.logical_and(b >= 4, b < 4 + GROUPS))
+            def _():
+                far_copy(b - 4).start()
+
+        @pl.when(b == 4)
         def _():
             for j in (2, 3):
                 for h in range(HEADS):
                     head_copy(j, h).start()
 
-        @pl.when(b == 8)
+        @pl.when(b == 9)
         def _():
             for w in weights:
                 w.start()
 
         return 0
 
-    def k_late(b, _):
-        slot = content(b)
-        k_tail(b, slot)
-        return 0
-
-    lax.fori_loop(0, 12, k_early, 0)
+    lax.fori_loop(3, 12, k_mid, 0)
     for h in range(HEADS):
         head_copy(2, h).wait()
         kn = jnp.dot(normed, wk[h], preferred_element_type=F32).astype(BF16).astype(F32)
@@ -238,6 +253,16 @@
             row = s * GROWS + h * PER
             new_score[row : row + PER, :] = sn[s * PER : s * PER + PER, :]
             new_value[row : row + PER, :] = vn[s * PER : s * PER + PER, :]
+    @pl.when(odd == 0)
+    def _():
+        for g in range(GROUPS):
+            pair_copy(g).wait()
+
+    def k_late(b, _):
+        slot = content(b)
+        refill(b, slot)
+        return 0
+
     lax.fori_loop(12, BATCH, k_late, 0)
 
     lane6 = lax.broadcasted_iota(jnp.int32, (HEADS, 128), 1)

time: 70.9 us -> 61.5 us (0.87)
  Pallas kernels: 69.3 us -> 60 us
    pallas_call x1, Pallas kernels: 69.3 us -> 60 us  [layer_step(): pl.pallas_call(fused_kernel, out_shape=jax.ShapeDtypeStruct((BATCH, D), B...]
where the time goes in v3:
time: 61.5 us; the launch traced here: 61.4 us
  Pallas kernels  60 us (98%)
  local copies, waits for them, and re-layouts  1.42 us (2%)
    pallas_call x1, Pallas kernels, layer_step(): pl.pallas_call(fused_kernel, out_shape=jax.ShapeDtypeStruct((BATCH, D), B...  60 us
    unnamed x1, local copies, waits for them, and re-layouts  1.42 us

profile of v3, /device:TPU:0, one launch (start us, length us, event | category | flops | bytes accessed | tf_op | source)
XLA Modules:
  0.0 61.4 jit_solution(4710616673823930395)
XLA Ops:
  0.0 60.0 %layer.1 = bf16[16,1536]{1,0:T(8,128)(2,1)} custom-call(s32[16]{0:T(128)} %len_ref.1, bf16[16,1536]{1,0:T(8,128)(2,1)} %x_hbm.1, bf16[1536]{0:T(1024)(128)(2,1)} %g1_hbm.1, bf16[1536]{0:T(1024)(128)(2,1)} %g2_hbm.1, bf16[6,128]{1,0:T(8,128)(2,1)} %u_hbm.1, bf16[6,128]{1,0:T(8,128)(2,1)} %wb_hbm.1, bf16[6,1536,128]{2,1,0:T(8,128)(2,1)} %bitcast.10, ...), custom_call_target="tpu_custom_call" | custom-call | tf_op jit(solution)/shard_map/layer/pallas_call | solution.py:432
  60.0 1.4 %copy.17 = bf16[16,1536]{1,0:T(8,128)(2,1)} copy(bf16[16,1536]{1,0:T(8,128)(2,1)} %layer.1) | data formatting | bytes 98304

commit v4 on v3

--- a/solution.py
+++ b/solution.py
@@ -32,10 +32,10 @@
 
 def fused_kernel(len_ref, x_hbm, g1_hbm, g2_hbm, u_hbm, wb_hbm, wq_hbm, wk_hbm, wv_hbm, rel_hbm, k_hbm, v_hbm, wo_hbm, wu_hbm, wd_hbm,
                  out_ref,
-                 xb, g1, g2, ub, wbb, wq, wk, wv, rel, qf, qc_ref, raw, new_score, new_value, new_prob,
+                 xb, g1, g2, ub, wbb, wq, wkv, kv, rel, qf, qc_ref, raw, new_score, new_value, new_prob,
                  ring, wo, wu, wd, score, rolled, from_pair, to_far, from_far, probs, stat_out, stat_in, ctx, ctx_in,
                  part_out, part_in, x1_ref, mlp_in,
-                 small_sem, in_sem, ring_sem, w_sem, pair_s, pair_r, far_s, far_r, stat_s, stat_r, ctx_s, ctx_r,
+                 small_sem, in_sem, kv_sem, kvp_s, kvp_r, ring_sem, w_sem, pair_s, pair_r, far_s, far_r, stat_s, stat_r, ctx_s, ctx_r,
                  part_s, part_r, mlp_s, mlp_r):
     tp, sp = lax.axis_index("tp"), lax.axis_index("sp")
     me = tp * 4 + sp
@@ -46,8 +46,11 @@
         ((x_hbm, xb), (g1_hbm, g1), (g2_hbm, g2), (u_hbm, ub), (wb_hbm, wbb)))]
 
     def head_copy(j, h):
-        a, b = ((wq_hbm, wq), (rel_hbm, rel), (wk_hbm, wk), (wv_hbm, wv))[j]
+        a, b = ((wq_hbm, wq), (rel_hbm, rel))[j]
         return pltpu.make_async_copy(a.at[h], b.at[h], in_sem.at[j, h])
+
+    def kv_load(src, j):
+        return pltpu.make_async_copy(src.at[lax.rem(sp, 2) * 3 + j], wkv.at[j], kv_sem.at[j])
 
     weights = (
         pltpu.make_async_copy(wo_hbm, wo, w_sem.at[0]),
@@ -69,6 +72,17 @@
     for j in range(2):
         for h in range(HEADS):
             head_copy(j, h).start()
+
+    @pl.when(sp < 2)
+    def _():
+        for j in range(3):
+            kv_load(wk_hbm, j).start()
+
+    @pl.when(sp >= 2)
+    def _():
+        for j in range(3):
+            kv_load(wv_hbm, j).start()
+
     for i in range(FIRST):
         pltpu.make_async_copy(k_hbm.at[i], ring.at[i], ring_sem.at[i]).start()
 
@@ -98,6 +112,12 @@
 
     def far_copy(g, src=None):
         return remote((to_far if src is None else src).at[:, rows(g), :], from_far.at[:, rows(g), :], far_s.at[g], far_r.at[g], tp, 3 - sp)
+
+    def kv_copy(ds, sending):
+        t, s = peer(0, ds)
+        _, fs = source(0, ds)
+        part = kv.at[pl.ds((sp if sending else fs) * 3, 3)]
+        return remote(part, part, kvp_s.at[ds - 1], kvp_r.at[ds - 1], t, s)
 
     def stat_copy(g, ds):
         t, s = peer(0, ds)
@@ -198,7 +218,9 @@
         def _():
             load(b + RING, slot)
 
-    pl.semaphore_wait(barrier, 7)
+    for j in range(3):
+        kv_load(wk_hbm, j).wait()
+        kv[sp * 3 + j] = jnp.dot(normed, wkv[j], preferred_element_type=F32).astype(BF16).astype(F32)
 
     def send(g):
         pair_copy(g).start()
@@ -212,6 +234,10 @@
         for k in range(4):
             roll(4 * b + k)
         refill(jnp.int32(b), slot)
+        if b == 0:
+            pl.semaphore_wait(barrier, 7)
+            for ds in range(1, 4):
+                kv_copy(ds, True).start()
         send(b)
     send(3)
 
@@ -229,12 +255,6 @@
             def _():
                 far_copy(b - 4).start()
 
-        @pl.when(b == 4)
-        def _():
-            for j in (2, 3):
-                for h in range(HEADS):
-                    head_copy(j, h).start()
-
         @pl.when(b == 9)
         def _():
             for w in weights:
@@ -243,16 +263,6 @@
         return 0
 
     lax.fori_loop(3, 12, k_mid, 0)
-    for h in range(HEADS):
-        head_copy(2, h).wait()
-        kn = jnp.dot(normed, wk[h], preferred_element_type=F32).astype(BF16).astype(F32)
-        head_copy(3, h).wait()
-        vn = jnp.dot(normed, wv[h], preferred_element_type=F32).astype(BF16).astype(F32)
-        sn = jnp.broadcast_to(jnp.sum(qc_ref[h] * kn, axis=1, keepdims=True), (BATCH, 128))
-        for s in range(GROUPS):
-            row = s * GROWS + h * PER
-            new_score[row : row + PER, :] = sn[s * PER : s * PER + PER, :]
-            new_value[row : row + PER, :] = vn[s * PER : s * PER + PER, :]
     @pl.when(odd == 0)
     def _():
         for g in range(GROUPS):
@@ -264,6 +274,15 @@
         return 0
 
     lax.fori_loop(12, BATCH, k_late, 0)
+    for ds in range(1, 4):
+        kv_copy(ds, True).wait_send()
+        kv_copy(ds, False).wait_recv()
+    for h in range(HEADS):
+        sn = jnp.broadcast_to(jnp.sum(qc_ref[h] * kv[h], axis=1, keepdims=True), (BATCH, 128))
+        for s in range(GROUPS):
+            row = s * GROWS + h * PER
+            new_score[row : row + PER, :] = sn[s * PER : s * PER + PER, :]
+            new_value[row : row + PER, :] = kv[HEADS + h, s * PER : s * PER + PER, :]
 
     lane6 = lax.broadcasted_iota(jnp.int32, (HEADS, 128), 1)
     head_row = lax.broadcasted_iota(jnp.int32, (HEADS, 128), 0)
@@ -395,9 +414,9 @@
         def _():
             project(g - 1)
 
-        @pl.when(jnp.logical_and(i == 1, g >= 2))
-        def _():
-            mlp(g - 2)
+        @pl.when(b == 9)
+        def _():
+            mlp(0)
 
         return 0
 
@@ -405,12 +424,14 @@
     attend(jnp.int32(BATCH - 2))
     project(GROUPS - 2)
     attend(jnp.int32(BATCH - 1))
-    send_ctx(GROUPS - 1)
-    mlp(GROUPS - 2)
-    project(GROUPS - 1)
-    done = [finish(0), finish(1)]
-    mlp(GROUPS - 1)
-    done = done + [finish(2), finish(3)]
+    send_ctx(3)
+    mlp(1)
+    project(3)
+    mlp(2)
+    done = [finish(0)]
+    mlp(3)
+    done = done + [finish(1), finish(2)]
+    done = done + [finish(3)]
     out_ref[...] = jnp.concatenate(done, axis=0).astype(BF16)
 
 
@@ -436,13 +457,13 @@
             out_specs=vm,
             scratch_shapes=[
                 VMEM((BATCH, D), BF16), VMEM((D,), BF16), VMEM((D,), BF16), VMEM((HEADS, HEAD), BF16), VMEM((HEADS, HEAD), BF16),
-                head_weight, head_weight, head_weight, VMEM((HEADS, BLK, HEAD), BF16),
+                head_weight, VMEM((3, D, HEAD), BF16), VMEM((2 * HEADS, BATCH, HEAD), F32), VMEM((HEADS, BLK, HEAD), BF16),
                 VMEM((HEADS, 128, 128), F32), VMEM((HEADS, BATCH, 128), F32), tiles, by_row, by_row, by_row,
                 VMEM((RING, HEADS, BLK, HEAD), BF16), VMEM((HEADS * HEAD, D), BF16), VMEM((D, HID), BF16), VMEM((HID, D), BF16),
                 tiles, tiles, tiles, tiles, tiles, VMEM((3, HEADS, BLK), F32),
                 by_row, VMEM((3, ROWS, 128), F32), by_row, VMEM((4, ROWS, 128), F32),
                 VMEM((GROUPS, PER, D), F32), VMEM((GROUPS, PER, D), F32), VMEM((GROUPS, PER, D), F32), VMEM((GROUPS, 8, PER, D), F32),
-                dma((5,)), dma((4, HEADS)), dma((RING,)), dma((3,)), dma((4,)), dma((4,)), dma((4,)), dma((4,)),
+                dma((5,)), dma((2, HEADS)), dma((3,)), dma((3,)), dma((3,)), dma((RING,)), dma((3,)), dma((4,)), dma((4,)), dma((4,)), dma((4,)),
                 dma((4, 3)), dma((4, 3)), dma((4, 3)), dma((4, 3)), dma((4,)), dma((4,)), dma((4, 7)), dma((4, 7)),
             ],
             compiler_params=pltpu.CompilerParams(vmem_limit_bytes=63 * 2**20, collective_id=0, has_side_effects=True),

time: 61.5 us -> 60.3 us (0.980)
  Pallas kernels: 60 us -> 58.7 us
    pallas_call x1, Pallas kernels: 60 us -> 58.7 us  [layer_step(): pl.pallas_call(fused_kernel, out_shape=jax.ShapeDtypeStruct((BATCH, D), B...]
where the time goes in v4:
time: 60.3 us; the launch traced here: 60.1 us
  Pallas kernels  58.7 us (97%)
  local copies, waits for them, and re-layouts  1.42 us (2%)
    pallas_call x1, Pallas kernels, layer_step(): pl.pallas_call(fused_kernel, out_shape=jax.ShapeDtypeStruct((BATCH, D), B...  58.7 us
    unnamed x1, local copies, waits for them, and re-layouts  1.42 us

profile of v4, /device:TPU:0, one launch (start us, length us, event | category | flops | bytes accessed | tf_op | source)
XLA Modules:
  0.0 60.1 jit_solution(7674393258754230777)
XLA Ops:
  0.0 58.7 %layer.1 = bf16[16,1536]{1,0:T(8,128)(2,1)} custom-call(s32[16]{0:T(128)} %len_ref.1, bf16[16,1536]{1,0:T(8,128)(2,1)} %x_hbm.1, bf16[1536]{0:T(1024)(128)(2,1)} %g1_hbm.1, bf16[1536]{0:T(1024)(128)(2,1)} %g2_hbm.1, bf16[6,128]{1,0:T(8,128)(2,1)} %u_hbm.1, bf16[6,128]{1,0:T(8,128)(2,1)} %wb_hbm.1, bf16[6,1536,128]{2,1,0:T(8,128)(2,1)} %bitcast.10, ...), custom_call_target="tpu_custom_call" | custom-call | tf_op jit(solution)/shard_map/layer/pallas_call | solution.py:453
  58.7 1.4 %copy.17 = bf16[16,1536]{1,0:T(8,128)(2,1)} copy(bf16[16,1536]{1,0:T(8,128)(2,1)} %layer.1) | data formatting | bytes 98304

commit v5 on v4

--- a/solution.py
+++ b/solution.py
@@ -21,7 +21,7 @@
 GROWS = HEADS * PER
 ROWS = GROUPS * GROWS
 RING = 8
-FIRST = 3
+FIRST = 5
 HID = 768
 
 
@@ -30,20 +30,20 @@
     return (wide * lax.rsqrt(mean_sq + EPS) * gain).astype(BF16)
 
 
-def fused_kernel(len_ref, x_hbm, g1_hbm, g2_hbm, u_hbm, wb_hbm, wq_hbm, wk_hbm, wv_hbm, rel_hbm, k_hbm, v_hbm, wo_hbm, wu_hbm, wd_hbm,
+def fused_kernel(len_hbm, x_hbm, g1_hbm, g2_hbm, u_hbm, wb_hbm, wq_hbm, wk_hbm, wv_hbm, rel_hbm, k_hbm, v_hbm, wo_hbm, wu_hbm, wd_hbm,
                  out_ref,
-                 xb, g1, g2, ub, wbb, wq, wkv, kv, rel, qf, qc_ref, raw, new_score, new_value, new_prob,
+                 len_ref, xb, g1, g2, ub, wbb, wq, wkv, kv, rel, qf, qc_ref, raw, new_score, new_value, new_prob,
                  ring, wo, wu, wd, score, rolled, from_pair, to_far, from_far, probs, stat_out, stat_in, ctx, ctx_in,
-                 part_out, part_in, x1_ref, mlp_in,
+                 part_out, part_in, x1_ref, mlp_in, x1_rows, rs_out, rs_in, ag,
                  small_sem, in_sem, kv_sem, kvp_s, kvp_r, ring_sem, w_sem, pair_s, pair_r, far_s, far_r, stat_s, stat_r, ctx_s, ctx_r,
-                 part_s, part_r, mlp_s, mlp_r):
+                 part_s, part_r, mlp_s, mlp_r, rs_s, rs_r, ag_s, ag_r):
     tp, sp = lax.axis_index("tp"), lax.axis_index("sp")
     me = tp * 4 + sp
     odd = lax.rem(sp, 2)
     pair = sp + 1 - 2 * odd
 
     small = [pltpu.make_async_copy(a, b, small_sem.at[i]) for i, (a, b) in enumerate(
-        ((x_hbm, xb), (g1_hbm, g1), (g2_hbm, g2), (u_hbm, ub), (wb_hbm, wbb)))]
+        ((len_hbm, len_ref), (x_hbm, xb), (g1_hbm, g1), (g2_hbm, g2), (u_hbm, ub), (wb_hbm, wbb)))]
 
     def head_copy(j, h):
         a, b = ((wq_hbm, wq), (rel_hbm, rel))[j]
@@ -83,7 +83,7 @@
         for j in range(3):
             kv_load(wv_hbm, j).start()
 
-    for i in range(FIRST):
+    for i in range(FIRST - 3):
         pltpu.make_async_copy(k_hbm.at[i], ring.at[i], ring_sem.at[i]).start()
 
     others = [(dt, ds) for dt in range(2) for ds in range(4) if (dt, ds) != (0, 0)]
@@ -137,6 +137,18 @@
         ft, fs = source(*others[j])
         slot = me if sending else ft * 4 + fs
         return remote(mlp_in.at[g, slot], mlp_in.at[g, slot], mlp_s.at[g, j], mlp_r.at[g, j], t, s)
+
+    def rs_copy(j, sending):
+        t, s = peer(*others[j])
+        ft, fs = source(*others[j])
+        slot = me if sending else ft * 4 + fs
+        return remote(rs_out.at[t * 4 + s], rs_in.at[slot], rs_s.at[j], rs_r.at[j], t, s)
+
+    def ag_copy(j, sending):
+        t, s = peer(*others[j])
+        ft, fs = source(*others[j])
+        slot = me if sending else ft * 4 + fs
+        return remote(ag.at[slot], ag.at[slot], ag_s.at[j], ag_r.at[j], t, s)
 
     for c in small:
         c.wait()
@@ -152,6 +164,9 @@
         qp = (q + wbb[h : h + 1, :].astype(F32)).astype(BF16)
         qc_ref[h] = qc
         qf[h, pl.ds(h, BATCH, stride=8), :] = qc
+        if h % 2 == 0:
+            i = FIRST - 3 + h // 2
+            pltpu.make_async_copy(k_hbm.at[i], ring.at[i], ring_sem.at[i]).start()
         head_copy(1, h).wait()
         by_dist = lax.dot_general(qp, rel[h], NT, preferred_element_type=F32)
         for c in range(TILES):
@@ -257,8 +272,7 @@
 
         @pl.when(b == 9)
         def _():
-            for w in weights:
-                w.start()
+            weights[0].start()
 
         return 0
 
@@ -363,23 +377,56 @@
         part_out[g] = jnp.dot(lhs, wo[...], preferred_element_type=F32)
         part_copy(g).start()
 
-    def mlp(g):
+    def middle(g):
         part_copy(g).wait()
-        x1 = (x1_ref[g] + (part_out[g] + part_in[g])).astype(BF16).astype(F32)
-        x1_ref[g] = x1
+        return (x1_ref[g] + (part_out[g] + part_in[g])).astype(BF16).astype(F32)
+
+    def hidden_layer(x1):
         up = jnp.dot(rms_norm(x1, g2[...].astype(F32).reshape(1, D)), wu[...], preferred_element_type=F32)
         act = jax.nn.gelu(up, approximate=True).astype(BF16)
-        mlp_in[g, me] = jnp.dot(act, wd[...], preferred_element_type=F32)
+        return jnp.dot(act, wd[...], preferred_element_type=F32)
+
+    def mlp(g):
+        x1 = middle(g)
+        x1_ref[g] = x1
+        mlp_in[g - 2, me] = hidden_layer(x1)
         for j in range(7):
-            mlp_copy(g, j, True).start()
+            mlp_copy(g - 2, j, True).start()
+
+    def first_mlp():
+        x1 = jnp.concatenate([middle(0), middle(1)], axis=0)
+        down = hidden_layer(x1)
+        for k in range(8):
+            x1_rows[k] = x1[k : k + 1, :]
+            rs_out[k] = down[k : k + 1, :]
+        for j in range(7):
+            rs_copy(j, True).start()
+        rs_in[me] = rs_out[me]
+
+    def first_sum():
+        for j in range(7):
+            rs_copy(j, True).wait_send()
+            rs_copy(j, False).wait_recv()
+        tot = rs_in[0]
+        for k in range(1, 8):
+            tot = tot + rs_in[k]
+        ag[me] = (x1_rows[me] + tot).astype(BF16).astype(F32)
+        for j in range(7):
+            ag_copy(j, True).start()
+
+    def first_finish():
+        for j in range(7):
+            ag_copy(j, True).wait_send()
+            ag_copy(j, False).wait_recv()
+        return [ag[k] for k in range(8)]
 
     def finish(g):
         for j in range(7):
-            mlp_copy(g, j, True).wait_send()
-            mlp_copy(g, j, False).wait_recv()
-        tot = mlp_in[g, 0]
+            mlp_copy(g - 2, j, True).wait_send()
+            mlp_copy(g - 2, j, False).wait_recv()
+        tot = mlp_in[g - 2, 0]
         for k in range(1, 8):
-            tot = tot + mlp_in[g, k]
+            tot = tot + mlp_in[g - 2, k]
         return x1_ref[g] + tot
 
     far_copy(0).wait()
@@ -399,8 +446,7 @@
 
         @pl.when(b == 3)
         def _():
-            for w in weights:
-                w.wait()
+            weights[0].wait()
 
         @pl.when(i == 1)
         def _():
@@ -414,9 +460,10 @@
         def _():
             project(g - 1)
 
-        @pl.when(b == 9)
-        def _():
-            mlp(0)
+        @pl.when(b == BATCH - RING - 1)
+        def _():
+            weights[1].start()
+            weights[2].start()
 
         return 0
 
@@ -425,12 +472,15 @@
     project(GROUPS - 2)
     attend(jnp.int32(BATCH - 1))
     send_ctx(3)
-    mlp(1)
+    weights[1].wait()
+    weights[2].wait()
+    first_mlp()
     project(3)
     mlp(2)
-    done = [finish(0)]
+    first_sum()
     mlp(3)
-    done = done + [finish(1), finish(2)]
+    done = first_finish()
+    done = done + [finish(2)]
     done = done + [finish(3)]
     out_ref[...] = jnp.concatenate(done, axis=0).astype(BF16)
 
@@ -442,7 +492,6 @@
     out_specs = spec_rows
     vm = pl.BlockSpec(memory_space=VMEM)
     hbm = pl.BlockSpec(memory_space=pl.ANY)
-    smem = pl.BlockSpec(memory_space=pltpu.SMEM)
     dma = pltpu.SemaphoreType.DMA
     head_weight = VMEM((HEADS, D, HEAD), BF16)
     tiles = VMEM((TILES, ROWS, 128), F32)
@@ -453,18 +502,19 @@
         return pl.pallas_call(
             fused_kernel,
             out_shape=jax.ShapeDtypeStruct((BATCH, D), BF16),
-            in_specs=[smem] + [hbm] * 14,
+            in_specs=[hbm] * 15,
             out_specs=vm,
             scratch_shapes=[
-                VMEM((BATCH, D), BF16), VMEM((D,), BF16), VMEM((D,), BF16), VMEM((HEADS, HEAD), BF16), VMEM((HEADS, HEAD), BF16),
+                pltpu.SMEM((BATCH,), jnp.int32), VMEM((BATCH, D), BF16), VMEM((D,), BF16), VMEM((D,), BF16), VMEM((HEADS, HEAD), BF16), VMEM((HEADS, HEAD), BF16),
                 head_weight, VMEM((3, D, HEAD), BF16), VMEM((2 * HEADS, BATCH, HEAD), F32), VMEM((HEADS, BLK, HEAD), BF16),
                 VMEM((HEADS, 128, 128), F32), VMEM((HEADS, BATCH, 128), F32), tiles, by_row, by_row, by_row,
                 VMEM((RING, HEADS, BLK, HEAD), BF16), VMEM((HEADS * HEAD, D), BF16), VMEM((D, HID), BF16), VMEM((HID, D), BF16),
                 tiles, tiles, tiles, tiles, tiles, VMEM((3, HEADS, BLK), F32),
                 by_row, VMEM((3, ROWS, 128), F32), by_row, VMEM((4, ROWS, 128), F32),
-                VMEM((GROUPS, PER, D), F32), VMEM((GROUPS, PER, D), F32), VMEM((GROUPS, PER, D), F32), VMEM((GROUPS, 8, PER, D), F32),
-                dma((5,)), dma((2, HEADS)), dma((3,)), dma((3,)), dma((3,)), dma((RING,)), dma((3,)), dma((4,)), dma((4,)), dma((4,)), dma((4,)),
-                dma((4, 3)), dma((4, 3)), dma((4, 3)), dma((4, 3)), dma((4,)), dma((4,)), dma((4, 7)), dma((4, 7)),
+                VMEM((GROUPS, PER, D), F32), VMEM((GROUPS, PER, D), F32), VMEM((GROUPS, PER, D), F32), VMEM((2, 8, PER, D), F32),
+                VMEM((8, 1, D), F32), VMEM((8, 1, D), F32), VMEM((8, 1, D), F32), VMEM((8, 1, D), F32),
+                dma((6,)), dma((2, HEADS)), dma((3,)), dma((3,)), dma((3,)), dma((RING,)), dma((3,)), dma((4,)), dma((4,)), dma((4,)), dma((4,)),
+                dma((4, 3)), dma((4, 3)), dma((4, 3)), dma((4, 3)), dma((4,)), dma((4,)), dma((2, 7)), dma((2, 7)), dma((7,)), dma((7,)), dma((7,)), dma((7,)),
             ],
             compiler_params=pltpu.CompilerParams(vmem_limit_bytes=63 * 2**20, collective_id=0, has_side_effects=True),
             name="layer",

time: 60.3 us -> 57.5 us (0.954)
  Pallas kernels: 58.7 us -> 56 us
    pallas_call x1, Pallas kernels: 58.7 us -> 56 us  [layer_step(): pl.pallas_call(fused_kernel, out_shape=jax.ShapeDtypeStruct((BATCH, D), B...]
where the time goes in v5:
time: 57.5 us; the launch traced here: 57.4 us
  Pallas kernels  56 us (97%)
  local copies, waits for them, and re-layouts  1.42 us (2%)
    pallas_call x1, Pallas kernels, layer_step(): pl.pallas_call(fused_kernel, out_shape=jax.ShapeDtypeStruct((BATCH, D), B...  56 us
    unnamed x1, local copies, waits for them, and re-layouts  1.42 us

profile of v5, /device:TPU:0, one launch (start us, length us, event | category | flops | bytes accessed | tf_op | source)
XLA Modules:
  0.0 57.4 jit_solution(9682882427304629789)
XLA Ops:
  0.0 56.0 %layer.1 = bf16[16,1536]{1,0:T(8,128)(2,1)} custom-call(s32[16]{0:T(128)} %len_hbm.1, bf16[16,1536]{1,0:T(8,128)(2,1)} %x_hbm.1, bf16[1536]{0:T(1024)(128)(2,1)} %g1_hbm.1, bf16[1536]{0:T(1024)(128)(2,1)} %g2_hbm.1, bf16[6,128]{1,0:T(8,128)(2,1)} %u_hbm.1, bf16[6,128]{1,0:T(8,128)(2,1)} %wb_hbm.1, bf16[6,1536,128]{2,1,0:T(8,128)(2,1)} %bitcast.10, ...), custom_call_target="tpu_custom_call" | custom-call | tf_op jit(solution)/shard_map/layer/pallas_call | solution.py:502
  56.0 1.4 %copy.17 = bf16[16,1536]{1,0:T(8,128)(2,1)} copy(bf16[16,1536]{1,0:T(8,128)(2,1)} %layer.1) | data formatting | bytes 98304

commit v6 on v5

--- a/solution.py
+++ b/solution.py
@@ -22,6 +22,7 @@
 ROWS = GROUPS * GROWS
 RING = 8
 FIRST = 5
+FIRST_SEND = 9
 HID = 768
 
 
@@ -323,7 +324,7 @@
         top = jnp.max(top, axis=1, keepdims=True)
         total = jnp.zeros((HEADS, 128), F32)
         at_new = jnp.zeros((HEADS, 128), F32)
-        slot = lax.rem(b, 3)
+        slot = lax.rem(b, 4)
         for c in range(TILES):
             pos = lane6 + 128 * c
             w = jnp.where(pos <= here, jnp.exp(sc[c] - top), 0.0)
@@ -338,7 +339,7 @@
     def attend(b):
         slot = lax.rem(b + BATCH, RING)
         pltpu.make_async_copy(v_hbm.at[b], ring.at[slot], ring_sem.at[slot]).wait()
-        pb = probs[lax.rem(b, 3)].astype(BF16)
+        pb = probs[lax.rem(b, 4)].astype(BF16)
         out = jnp.zeros((HEADS, 128), F32)
         for p in range(HEADS // 2):
             values = jnp.concatenate([ring[slot, 2 * p], ring[slot, 2 * p + 1]], axis=1)
@@ -432,33 +433,34 @@
     far_copy(0).wait()
     softmax(0)
     softmax(1)
+    softmax(2)
 
     def v_step(b, _):
         g, i = lax.div(b, PER), lax.rem(b, PER)
 
-        @pl.when(jnp.logical_and(i == 2, g < GROUPS - 1))
+        @pl.when(jnp.logical_and(i == 1, g < GROUPS - 1))
         def _():
             far_copy(g + 1).wait()
 
         slot = attend(b)
-        softmax(b + 2)
+        softmax(b + 3)
         load(b + BATCH + RING, slot)
 
         @pl.when(b == 3)
         def _():
             weights[0].wait()
 
-        @pl.when(i == 1)
+        @pl.when(i == 0)
         def _():
             send_stats(g)
 
-        @pl.when(i == 3)
-        def _():
-            send_ctx(g)
-
-        @pl.when(jnp.logical_and(i == 2, g >= 1))
-        def _():
-            project(g - 1)
+        @pl.when(jnp.logical_and(b >= FIRST_SEND, b < FIRST_SEND + GROUPS - 1))
+        def _():
+            send_ctx(b - FIRST_SEND)
+
+        @pl.when(jnp.logical_and(b >= FIRST_SEND + 3, b < BATCH - 3))
+        def _():
+            project(b - FIRST_SEND - 3)
 
         @pl.when(b == BATCH - RING - 1)
         def _():
@@ -467,7 +469,9 @@
 
         return 0
 
-    lax.fori_loop(0, BATCH - 2, v_step, 0)
+    lax.fori_loop(0, BATCH - 3, v_step, 0)
+    attend(jnp.int32(BATCH - 3))
+    project(GROUPS - 3)
     attend(jnp.int32(BATCH - 2))
     project(GROUPS - 2)
     attend(jnp.int32(BATCH - 1))
@@ -509,7 +513,7 @@
                 head_weight, VMEM((3, D, HEAD), BF16), VMEM((2 * HEADS, BATCH, HEAD), F32), VMEM((HEADS, BLK, HEAD), BF16),
                 VMEM((HEADS, 128, 128), F32), VMEM((HEADS, BATCH, 128), F32), tiles, by_row, by_row, by_row,
                 VMEM((RING, HEADS, BLK, HEAD), BF16), VMEM((HEADS * HEAD, D), BF16), VMEM((D, HID), BF16), VMEM((HID, D), BF16),
-                tiles, tiles, tiles, tiles, tiles, VMEM((3, HEADS, BLK), F32),
+                tiles, tiles, tiles, tiles, tiles, VMEM((4, HEADS, BLK), F32),
                 by_row, VMEM((3, ROWS, 128), F32), by_row, VMEM((4, ROWS, 128), F32),
                 VMEM((GROUPS, PER, D), F32), VMEM((GROUPS, PER, D), F32), VMEM((GROUPS, PER, D), F32), VMEM((2, 8, PER, D), F32),
                 VMEM((8, 1, D), F32), VMEM((8, 1, D), F32), VMEM((8, 1, D), F32), VMEM((8, 1, D), F32),

time: 57.5 us -> 53 us (0.922)
  Pallas kernels: 56 us -> 51.4 us
    pallas_call x1, Pallas kernels: 56 us -> 51.4 us  [layer_step(): pl.pallas_call(fused_kernel, out_shape=jax.ShapeDtypeStruct((BATCH, D), B...]
where the time goes in v6:
time: 53 us; the launch traced here: 52.8 us
  Pallas kernels  51.4 us (97%)
  local copies, waits for them, and re-layouts  1.42 us (3%)
    pallas_call x1, Pallas kernels, layer_step(): pl.pallas_call(fused_kernel, out_shape=jax.ShapeDtypeStruct((BATCH, D), B...  51.4 us
    unnamed x1, local copies, waits for them, and re-layouts  1.42 us

profile of v6, /device:TPU:0, one launch (start us, length us, event | category | flops | bytes accessed | tf_op | source)
XLA Modules:
  0.0 52.8 jit_solution(442196565321031953)
XLA Ops:
  0.0 51.4 %layer.1 = bf16[16,1536]{1,0:T(8,128)(2,1)} custom-call(s32[16]{0:T(128)} %len_hbm.1, bf16[16,1536]{1,0:T(8,128)(2,1)} %x_hbm.1, bf16[1536]{0:T(1024)(128)(2,1)} %g1_hbm.1, bf16[1536]{0:T(1024)(128)(2,1)} %g2_hbm.1, bf16[6,128]{1,0:T(8,128)(2,1)} %u_hbm.1, bf16[6,128]{1,0:T(8,128)(2,1)} %wb_hbm.1, bf16[6,1536,128]{2,1,0:T(8,128)(2,1)} %bitcast.10, ...), custom_call_target="tpu_custom_call" | custom-call | tf_op jit(solution)/shard_map/layer/pallas_call | solution.py:506
  51.4 1.4 %copy.17 = bf16[16,1536]{1,0:T(8,128)(2,1)} copy(bf16[16,1536]{1,0:T(8,128)(2,1)} %layer.1) | data formatting | bytes 98304

commit v7 on v6

--- a/solution.py
+++ b/solution.py
@@ -21,7 +21,7 @@
 GROWS = HEADS * PER
 ROWS = GROUPS * GROWS
 RING = 8
-FIRST = 5
+FIRST = 6
 FIRST_SEND = 9
 HID = 768
 

time: 53 us -> 53.7 us (1.013)
  Pallas kernels: 51.4 us -> 52.1 us
    pallas_call x1, Pallas kernels: 51.4 us -> 52.1 us  [layer_step(): pl.pallas_call(fused_kernel, out_shape=jax.ShapeDtypeStruct((BATCH, D), B...]
where the time goes in v7:
time: 53.7 us; the launch traced here: 53.5 us
  Pallas kernels  52.1 us (97%)
  local copies, waits for them, and re-layouts  1.42 us (3%)
    pallas_call x1, Pallas kernels, layer_step(): pl.pallas_call(fused_kernel, out_shape=jax.ShapeDtypeStruct((BATCH, D), B...  52.1 us
    unnamed x1, local copies, waits for them, and re-layouts  1.42 us

profile of v7, /device:TPU:0, one launch (start us, length us, event | category | flops | bytes accessed | tf_op | source)
XLA Modules:
  0.0 53.5 jit_solution(1366495087500331868)
XLA Ops:
  0.0 52.1 %layer.1 = bf16[16,1536]{1,0:T(8,128)(2,1)} custom-call(s32[16]{0:T(128)} %len_hbm.1, bf16[16,1536]{1,0:T(8,128)(2,1)} %x_hbm.1, bf16[1536]{0:T(1024)(128)(2,1)} %g1_hbm.1, bf16[1536]{0:T(1024)(128)(2,1)} %g2_hbm.1, bf16[6,128]{1,0:T(8,128)(2,1)} %u_hbm.1, bf16[6,128]{1,0:T(8,128)(2,1)} %wb_hbm.1, bf16[6,1536,128]{2,1,0:T(8,128)(2,1)} %bitcast.10, ...), custom_call_target="tpu_custom_call" | custom-call | tf_op jit(solution)/shard_map/layer/pallas_call | solution.py:506
  52.1 1.4 %copy.17 = bf16[16,1536]{1,0:T(8,128)(2,1)} copy(bf16[16,1536]{1,0:T(8,128)(2,1)} %layer.1) | data formatting | bytes 98304
